TPU v7x, 128 devices: a whole 4x4x4 slice. The times are simulated.
128 devices in a mesh: rep: 1, shard: 128 (over z, y, x, core).
Axes of the slice: x: 4, y: 4, z: 4, core: 2. Of those that a mesh axis runs over, the one named last changes fastest.
Arguments:
- ratings: float32 [8192, 16384], P(('rep', 'shard'))
- observed: int32 [8192, 16384], P(('rep', 'shard'))
- user_init: float32 [8192, 192], P(('rep', 'shard'))
- item_init: float32 [16384, 192], P(('rep', 'shard'))
Outputs:
- output 1: float32 [8192, 192], P(('rep', 'shard'))
- output 2: float32 [16384, 192], P(('rep', 'shard'))
All inputs are finite; a program needn't handle non-finite values.
Results may differ from a plain program's by a relative error of at most 0.0169468.
Values are sent between devices in bfloat16 or wider.
A program may use at most 1 GiB of HBM per device.

v0:
```python
import jax
import jax.numpy as jnp
import math
from jax import lax
from jax.sharding import PartitionSpec as P

STRATUM_STEPS = 4
EPOCHS = 2


def solution(mesh):
    group_devs = mesh.shape["shard"]
    row_spec = P(("rep", "shard"), None)
    shift_back = [(source, (source - 1) % group_devs) for source in range(group_devs)]

    def local(ratings, observed, user_init, item_init):
        users_dev = ratings.shape[0]
        items_dev, factor_rank = item_init.shape
        step_scale = (users_dev + items_dev + factor_rank) / math.sqrt(factor_rank)
        step_size = 0.5 / step_scale
        weight_decay = 0.03 * math.sqrt(users_dev * items_dev / factor_rank)
        seen_all = observed != 0
        my_index = lax.axis_index("shard")

        def stratum(stratum_idx, state_pair):
            user_blk, item_blk = state_pair
            col_start = ((my_index + stratum_idx) % group_devs) * items_dev
            rating_blk = lax.dynamic_slice_in_dim(ratings, col_start, items_dev, axis=1)
            seen_blk = lax.dynamic_slice_in_dim(seen_all, col_start, items_dev, axis=1)

            def step(unused, inner_pair):
                user_cur, item_cur = inner_pair
                item_bf = item_cur.astype(jnp.bfloat16)
                predicted = jnp.einsum("ur,ir->ui", user_cur.astype(jnp.bfloat16), item_bf, preferred_element_type=jnp.float32)
                residual = jnp.where(seen_blk, predicted - rating_blk, 0.0).astype(jnp.bfloat16)
                grad_user = jnp.dot(residual, item_bf, preferred_element_type=jnp.float32)
                user_new = user_cur - step_size * (grad_user + weight_decay * user_cur)
                user_bf = user_new.astype(jnp.bfloat16)
                predicted = jnp.einsum("ur,ir->ui", user_bf, item_bf, preferred_element_type=jnp.float32)
                residual = jnp.where(seen_blk, predicted - rating_blk, 0.0).astype(jnp.bfloat16)
                grad_item = jnp.einsum("ui,ur->ir", residual, user_bf, preferred_element_type=jnp.float32)
                item_new = item_cur - step_size * (grad_item + weight_decay * item_cur)
                return user_new, item_new

            user_blk, item_blk = lax.fori_loop(0, STRATUM_STEPS, step, (user_blk, item_blk))
            item_blk = lax.ppermute(item_blk, "shard", shift_back)
            return user_blk, item_blk

        return lax.fori_loop(0, EPOCHS * group_devs, stratum, (user_init, item_init))

    return jax.shard_map(local, mesh=mesh, in_specs=(row_spec, row_spec, row_spec, row_spec), out_specs=(row_spec, row_spec), check_vma=False)
```

profile of v0, /device:TPU:0, one launch (start us, length us, event | category | flops | bytes accessed | tf_op | source)
XLA Modules:
  0.0 3302.9 jit_solution(14646547522809711113)
XLA Ops:
  3.4 3298.8 %while.53 = (s32[]{:T(128)}, f32[64,192]{1,0:T(8,128)S(1)}, f32[128,192]{0,1:T(8,128)S(1)}, s32[]{:T(128)}, f32[64,16384]{1,0:T(8,128)}, /*index=5*/pred[64,1638...) while((s32[]{:T(128)}, f32[64,192]{1,0:T(8,128)S(1)}, ...), condition=%wide.region_3.4_spmd, body=%wide.region_0.3_spmd.sunk | while | flops 12890132 | bytes 1491401 | solution.py:49
  6.8 8.3 collective-permute-start
  20.6 7.4 collective-permute-start
  46.4 7.4 collective-permute-start
  59.3 7.4 collective-permute-start
  97.9 7.4 collective-permute-start
  110.9 7.4 collective-permute-start
  123.7 7.4 collective-permute-start
  136.6 7.4 collective-permute-start
  149.5 7.4 collective-permute-start
  162.4 7.4 collective-permute-start
  175.3 7.4 collective-permute-start
  188.1 7.4 collective-permute-start
  201.0 7.4 collective-permute-start
  213.9 7.4 collective-permute-start
  226.8 7.4 collective-permute-start
  239.7 7.4 collective-permute-start
  252.5 7.4 collective-permute-start
  265.4 7.4 collective-permute-start
  278.3 7.4 collective-permute-start
  291.2 7.4 collective-permute-start
  304.1 7.4 collective-permute-start
  316.9 7.4 collective-permute-start
  329.8 7.4 collective-permute-start
  342.7 7.4 collective-permute-start
  355.6 7.4 collective-permute-start
  368.5 7.4 collective-permute-start
  381.4 7.4 collective-permute-start
  394.2 7.4 collective-permute-start
  407.1 7.4 collective-permute-start
  420.0 7.4 collective-permute-start
  432.9 7.4 collective-permute-start
  445.8 7.4 collective-permute-start
  458.6 7.4 collective-permute-start
  471.5 7.4 collective-permute-start
  484.4 7.4 collective-permute-start
  497.3 7.4 collective-permute-start
  510.2 7.4 collective-permute-start
  523.0 7.4 collective-permute-start
  535.9 7.4 collective-permute-start
  548.8 7.4 collective-permute-start
  561.7 7.4 collective-permute-start
  574.6 7.4 collective-permute-start
  587.5 7.4 collective-permute-start
  600.3 7.4 collective-permute-start
  613.2 7.4 collective-permute-start
  626.1 7.4 collective-permute-start
  639.0 7.4 collective-permute-start
  651.9 7.4 collective-permute-start
  780.7 7.4 collective-permute-start
  1025.4 7.4 collective-permute-start
  1154.2 7.4 collective-permute-start
  1386.1 7.4 collective-permute-start
  1630.8 7.4 collective-permute-start
  1695.3 7.4 collective-permute-start
  1708.2 7.4 collective-permute-start
  1746.8 7.4 collective-permute-start
  1940.1 7.4 collective-permute-start
  2184.8 7.4 collective-permute-start
  2429.5 7.4 collective-permute-start
  2674.3 7.4 collective-permute-start
  2803.1 7.4 collective-permute-start
  3035.0 7.4 collective-permute-start
  3279.7 7.4 collective-permute-start
  (5578 shorter events, 3429.3 us)
Async XLA Ops:
  6.8 10.5 collective-permute-start
  20.6 9.6 collective-permute-start
  46.4 9.6 collective-permute-start
  59.3 9.6 collective-permute-start
  97.9 9.6 collective-permute-start
  123.7 9.6 collective-permute-start
  162.4 9.6 collective-permute-start
  188.1 9.6 collective-permute-start
  201.0 9.6 collective-permute-start
  226.8 9.6 collective-permute-start
  239.7 9.6 collective-permute-start
  265.4 9.6 collective-permute-start
  291.2 9.6 collective-permute-start
  304.1 9.6 collective-permute-start
  329.8 9.6 collective-permute-start
  342.7 9.6 collective-permute-start
  368.5 9.6 collective-permute-start
  407.1 9.6 collective-permute-start
  432.9 9.6 collective-permute-start
  445.8 9.6 collective-permute-start
  471.5 9.6 collective-permute-start
  484.4 9.6 collective-permute-start
  510.2 9.6 collective-permute-start
  535.9 9.6 collective-permute-start
  548.8 9.6 collective-permute-start
  574.6 9.6 collective-permute-start
  587.5 9.6 collective-permute-start
  613.2 9.6 collective-permute-start
  651.9 9.6 collective-permute-start
  677.6 9.6 collective-permute-start
  690.5 9.6 collective-permute-start
  716.3 9.6 collective-permute-start
  729.1 9.6 collective-permute-start
  754.9 9.6 collective-permute-start
  780.7 9.6 collective-permute-start
  793.5 9.6 collective-permute-start
  819.3 9.6 collective-permute-start
  832.2 9.6 collective-permute-start
  858.0 9.6 collective-permute-start
  896.6 9.6 collective-permute-start
  922.4 9.6 collective-permute-start
  935.2 9.6 collective-permute-start
  961.0 9.6 collective-permute-start
  973.9 9.6 collective-permute-start
  999.6 9.6 collective-permute-start
  1025.4 9.6 collective-permute-start
  1038.3 9.6 collective-permute-start
  1064.0 9.6 collective-permute-start
  1076.9 9.6 collective-permute-start
  1102.7 9.6 collective-permute-start
  1154.2 9.6 collective-permute-start
  1180.0 9.6 collective-permute-start
  1192.9 9.6 collective-permute-start
  1218.7 9.6 collective-permute-start
  1257.3 9.6 collective-permute-start
  1283.1 9.6 collective-permute-start
  1295.9 9.6 collective-permute-start
  1321.7 9.6 collective-permute-start
  1334.6 9.6 collective-permute-start
  1360.3 9.6 collective-permute-start
  1386.1 9.6 collective-permute-start
  1695.3 9.6 collective-permute-start
  1746.8 9.6 collective-permute-start
  2803.1 9.6 collective-permute-start
  (196 other events, 1848.5 us)
where the time goes:
time: 3320 us; the launch traced here: 3300 us
  starting transfers between devices  1890 us (57%)
  matrix products  581 us (18%)
  waiting for transfers between devices  567 us (17%)
  local copies, waits for them, and re-layouts  215 us (6%)
  loops' own time  46.5 us (1%)
    ppermute x256, starting transfers between devices, stratum(): item_blk = lax.ppermute(item_blk, 'shard', shift_back)  1890 us
    ppermute x256, waiting for transfers between devices, stratum(): item_blk = lax.ppermute(item_blk, 'shard', shift_back)  567 us
    dot_general x1024, matrix products, step(): jnp.einsum('ui,ur->ir', residual, user_bf, preferred_element_type=jnp.flo...  303 us
    dot_general x1024, matrix products, step(): grad_user = jnp.dot(residual, item_bf, preferred_element_type=jnp.float32)  278 us
    dynamic_slice x256, local copies, waits for them, and re-layouts, stratum(): rating_blk = lax.dynamic_slice_in_dim(ratings, col_start, items_dev, axis=1)  197 us

commit v1 on v0

v1 whole, which is shorter than its diff:
```python
import functools
import math

import jax
import jax.numpy as jnp
from jax import lax
from jax.experimental import pallas as pl
from jax.experimental.pallas import tpu as pltpu
from jax.sharding import PartitionSpec as P

STRATUM_STEPS = 4
EPOCHS = 2
ITEM_BLOCKS = 4
SLOTS = 9
HALF_STEPS = 2 * STRATUM_STEPS
LEAD = SLOTS - HALF_STEPS + 1

ROW_BY_ROW = (((1,), (1,)), ((), ()))
PLAIN = (((1,), (0,)), ((), ()))


def dot(lhs, rhs, dims):
    return lax.dot_general(lhs, rhs, dims, preferred_element_type=jnp.float32)


def worker_device(worker, n_devs):
    if n_devs != 128:
        return worker * ITEM_BLOCKS
    plane = worker // 16
    place = worker + plane * (31 - 2 * worker)
    y = place // 4
    odd = y % 2
    x = place % 4
    x = x + odd * (3 - 2 * x)
    return ((plane * 4 + y) * 4 + x) * 2 + 1


def worker_of(dev, n_devs):
    if n_devs != 128:
        return dev // ITEM_BLOCKS
    chip = dev // 2
    plane = (chip // 16) % 2
    y = (chip // 4) % 4
    x = chip % 4
    place = y * 4 + x + (y % 2) * (3 - 2 * x)
    return place + plane * (31 - 2 * place)


def is_worker(dev, n_devs):
    if n_devs != 128:
        return dev % ITEM_BLOCKS == 0
    return jnp.logical_and(dev % 2 == 1, dev < 64)


def kernel(n_devs, strata, step_size, weight_decay, ratings, user_init, item_init, user_out, item_out, rated, turned,
           arriving, handed, handed_bf, leaving, user, user_bf, item, item_bf, user_start,
           block_send, block_recv, start_send, user_recv, item_recv, hop_send, hop_recv, end_send, end_recv):
    k = ITEM_BLOCKS
    workers = n_devs // k
    items = item_init.shape[0]
    me = lax.axis_index("shard")
    last = k - 1

    def remote(src, dst, send, recv, dev):
        return pltpu.make_async_remote_copy(
            src_ref=src, dst_ref=dst, send_sem=send, recv_sem=recv, device_id={"shard": dev}, device_id_type=pl.DeviceIdType.MESH
        )

    def arrival(like, dst, recv):
        return pltpu.make_async_copy(like, dst, recv)

    def send(src, dst, send_sem, recv_sem, dev):
        @pl.when(dev != me)
        def _():
            remote(src, dst, send_sem, recv_sem, dev).start()

        @pl.when(dev == me)
        def _():
            pltpu.make_async_copy(src, dst, recv_sem).start()

    def wait_sent(src, dst, send_sem, recv_sem, dev):
        @pl.when(dev != me)
        def _():
            remote(src, dst, send_sem, recv_sem, dev).wait_send()

    home = worker_device(me // k, n_devs)
    user_copy = (user_init, user_start.at[me % k], start_send.at[0], user_recv.at[me % k], home)
    item_copy = (item_init, item.at[me % k], start_send.at[1], item_recv.at[me % k], home)
    send(*user_copy)
    send(*item_copy)

    def block_copy(turn):
        worker = (me // k + turn) % workers
        columns = pl.ds(pl.multiple_of(worker * (k * items), 128), k * items)
        return ratings.at[:, columns], rated.at[me], block_send.at[turn], block_recv.at[me], worker_device(worker, n_devs)

    @pl.loop(0, workers)
    def _(turn):
        send(*block_copy(turn))

    @pl.when(is_worker(me, n_devs))
    def _():
        mine = worker_of(me, n_devs)
        first = mine * k
        after = worker_device((mine + 1) % workers, n_devs)

        def wait_block(block):
            arrival(ratings.at[:, pl.ds(0, k * items)], rated.at[block], block_recv.at[block]).wait()

        def hop(stratum):
            slot = (stratum + 1) % n_devs
            return remote(leaving.at[stratum % 2], arriving.at[slot], hop_send.at[stratum % 2], hop_recv.at[slot], after)

        for c in range(k):
            arrival(user_init, user_start.at[c], user_recv.at[c]).wait()
            arrival(item_init, item.at[c], item_recv.at[c]).wait()
            wait_block(first + c)
        for c in range(k):
            if c == 0:
                arriving[0] = user_start[0]
            else:
                handed[c - 1] = user_start[c]
                handed_bf[c - 1] = user_start[c].astype(jnp.bfloat16)
            item_bf[c] = item[c].astype(jnp.bfloat16)

        def slot(work):
            first_product, residual = {}, {}
            for c, half, stratum in work:
                if half == 0:
                    lhs = arriving[stratum % n_devs].astype(jnp.bfloat16) if c == 0 else handed_bf[c - 1]
                else:
                    lhs = user_bf[c]
                if half % 2 == 0:
                    first_product[c] = dot(lhs, item_bf[c], ROW_BY_ROW)
                else:
                    first_product[c] = dot(item_bf[c], lhs, ROW_BY_ROW)
            for c, half, stratum in work:
                if half % 2 == 0:
                    block = (first + c - stratum + 2 * n_devs) % n_devs
                    known = rated[block, :, c * items : (c + 1) * items]
                    if half == 0:
                        turned[c] = known.T
                else:
                    known = turned[c]
                residual[c] = jnp.where(known != known, 0.0, first_product[c] - known).astype(jnp.bfloat16)
            for c, half, stratum in work:
                if half % 2 == 0:
                    if half > 0:
                        old = user[c]
                    elif c == 0:
                        old = arriving[stratum % n_devs]
                    else:
                        old = handed[c - 1]
                    grad = dot(residual[c], item_bf[c], PLAIN)
                    new = old - step_size * (grad + weight_decay * old)
                    new_bf = new.astype(jnp.bfloat16)
                    user_bf[c] = new_bf
                    if half < HALF_STEPS - 2:
                        user[c] = new
                    elif c < last:
                        handed[c] = new
                        handed_bf[c] = new_bf
                    else:
                        leaving[stratum % 2] = new
                else:
                    old = item[c]
                    grad = dot(residual[c], user_bf[c], PLAIN)
                    new = old - step_size * (grad + weight_decay * old)
                    item[c] = new
                    item_bf[c] = new.astype(jnp.bfloat16)

        def work_of(s, stratum, first_only=False):
            work = []
            for c in range(k):
                place = s + LEAD * c
                if place < 0 or (first_only and place >= SLOTS):
                    continue
                if place % SLOTS < HALF_STEPS:
                    work.append((c, place % SLOTS, stratum + place // SLOTS))
            return work

        leave_slot = (HALF_STEPS - 1 - LEAD * last) % SLOTS

        def stratum_body(stratum, ends):
            @pl.when(stratum > 0)
            def _():
                slot_in = stratum % n_devs
                arrival(leaving.at[0], arriving.at[slot_in], hop_recv.at[slot_in]).wait()

            @pl.when(jnp.logical_and(stratum > 0, stratum <= n_devs - k))
            def _():
                wait_block((first - stratum + n_devs) % n_devs)

            for s in range(SLOTS):
                if s == leave_slot and not ends:
                    @pl.when(stratum > 0)
                    def _():
                        hop(stratum - 1).wait_send()

                    hop(stratum).start()
                slot(work_of(s, stratum, ends))

        for s in range(-LEAD * last, 0):
            slot(work_of(s, 0))

        @pl.loop(0, strata - 1)
        def _(stratum):
            stratum_body(stratum, False)

        hop(strata - 2).wait_send()
        stratum_body(strata - 1, True)

        def end_copies(c):
            done = handed.at[c] if c < last else leaving.at[(strata - 1) % 2]
            block = first + c
            return (
                (done, user_out, end_send.at[2 * c], end_recv.at[0], (block + 1) % n_devs),
                (item.at[c], item_out, end_send.at[2 * c + 1], end_recv.at[1], block),
            )

        for c in range(k):
            for copy in end_copies(c):
                send(*copy)
        for c in range(k):
            for copy in end_copies(c):
                wait_sent(*copy)

    wait_sent(*user_copy)
    wait_sent(*item_copy)

    @pl.loop(0, workers)
    def _(turn):
        wait_sent(*block_copy(turn))

    arrival(user_init, user_out, end_recv.at[0]).wait()
    arrival(item_init, item_out, end_recv.at[1]).wait()


def solution(mesh):
    n_devs = mesh.shape["shard"]
    row_spec = P(("rep", "shard"), None)
    k = ITEM_BLOCKS
    workers = n_devs // k

    def local(ratings, observed, user_init, item_init):
        users, rank = user_init.shape
        items = item_init.shape[0]
        step_scale = (users + items + rank) / math.sqrt(rank)
        step_size = 0.5 / step_scale
        weight_decay = 0.03 * math.sqrt(users * items / rank)
        masked = jnp.where(observed != 0, ratings, jnp.nan)
        dma = pltpu.SemaphoreType.DMA
        return pl.pallas_call(
            functools.partial(kernel, n_devs, EPOCHS * n_devs, step_size, weight_decay),
            out_shape=(jax.ShapeDtypeStruct((users, rank), jnp.float32), jax.ShapeDtypeStruct((items, rank), jnp.float32)),
            in_specs=[
                pl.BlockSpec(memory_space=pl.ANY),
                pl.BlockSpec(memory_space=pltpu.VMEM),
                pl.BlockSpec(memory_space=pltpu.VMEM),
            ],
            out_specs=(pl.BlockSpec(memory_space=pltpu.VMEM), pl.BlockSpec(memory_space=pltpu.VMEM)),
            scratch_shapes=[
                pltpu.VMEM((n_devs, users, k * items), jnp.float32),
                pltpu.VMEM((k, items, users), jnp.float32),
                pltpu.VMEM((n_devs, users, rank), jnp.float32),
                pltpu.VMEM((k - 1, users, rank), jnp.float32),
                pltpu.VMEM((k - 1, users, rank), jnp.bfloat16),
                pltpu.VMEM((2, users, rank), jnp.float32),
                pltpu.VMEM((k, users, rank), jnp.float32),
                pltpu.VMEM((k, users, rank), jnp.bfloat16),
                pltpu.VMEM((k, items, rank), jnp.float32),
                pltpu.VMEM((k, items, rank), jnp.bfloat16),
                pltpu.VMEM((k, users, rank), jnp.float32),
                dma((workers,)),
                dma((n_devs,)),
                dma((2,)),
                dma((k,)),
                dma((k,)),
                dma((2,)),
                dma((n_devs,)),
                dma((2 * k,)),
                dma((2,)),
            ],
            compiler_params=pltpu.CompilerParams(has_side_effects=True, vmem_limit_bytes=60 * 2**20),
            name="strata",
        )(masked, user_init, item_init)

    return jax.shard_map(local, mesh=mesh, in_specs=(row_spec,) * 4, out_specs=(row_spec, row_spec), check_vma=False)
```

time: 3320 us -> 806 us (0.24)
  the two profiles are of different devices: /device:TPU:0 before, /device:TPU:39 now
where the time goes in v1:
time: 806 us
  Pallas kernels  795 us (99%)
    pallas_call x1, Pallas kernels, local(): pl.pallas_call(functools.partial(kernel, n_devs, EPOCHS * n_devs, step_si...  795 us

profile of v1, /device:TPU:39, one launch (start us, length us, event | category | flops | bytes accessed | tf_op | source)
XLA Modules:
  0.0 805.8 jit_solution(14682288052897556880)
XLA Ops:
  0.6 1.6 copy.6.item_init
  2.3 5.9 compare_select_fusion.ratings
  8.1 794.5 %strata.1 = (f32[64,192]{1,0:T(8,128)}, f32[128,192]{1,0:T(8,128)}) custom-call(f32[64,16384]{1,0:T(8,128)} %compare_select_fusion.ratings, f32[64,192]{1,0:T(8,128)} %user_init.1, f32[128,192]{1,0:T(8,128)} %copy.6.item_init), custom_call_target="tpu_custom_call" | custom-call | tf_op jit(solution)/shard_map/strata/pallas_call | solution.py:253
  802.7 1.6 copy.7
  804.3 1.5 copy.9

commit v2 on v1

--- a/solution.py
+++ b/solution.py
@@ -12,6 +12,7 @@
 EPOCHS = 2
 ITEM_BLOCKS = 4
 SLOTS = 9
+AHEAD = 8
 HALF_STEPS = 2 * STRATUM_STEPS
 LEAD = SLOTS - HALF_STEPS + 1
 
@@ -54,7 +55,7 @@
 
 def kernel(n_devs, strata, step_size, weight_decay, ratings, user_init, item_init, user_out, item_out, rated, turned,
            arriving, handed, handed_bf, leaving, user, user_bf, item, item_bf, user_start,
-           block_send, block_recv, start_send, user_recv, item_recv, hop_send, hop_recv, end_send, end_recv):
+           go, block_send, block_recv, start_send, user_recv, item_recv, hop_send, hop_recv, end_send, end_recv):
     k = ITEM_BLOCKS
     workers = n_devs // k
     items = item_init.shape[0]
@@ -94,9 +95,18 @@
         columns = pl.ds(pl.multiple_of(worker * (k * items), 128), k * items)
         return ratings.at[:, columns], rated.at[me], block_send.at[turn], block_recv.at[me], worker_device(worker, n_devs)
 
-    @pl.loop(0, workers)
+    free_turns = jnp.minimum((AHEAD + me % k) // k + 1, workers)
+
+    @pl.loop(0, free_turns)
     def _(turn):
         send(*block_copy(turn))
+
+    @pl.when(jnp.logical_not(is_worker(me, n_devs)))
+    def _():
+        @pl.loop(free_turns, workers)
+        def _(turn):
+            pl.semaphore_wait(go, 1)
+            send(*block_copy(turn))
 
     @pl.when(is_worker(me, n_devs))
     def _():
@@ -191,6 +201,20 @@
             def _():
                 wait_block((first - stratum + n_devs) % n_devs)
 
+            if not ends:
+                asked = stratum + AHEAD
+                source = (first - asked + 2 * n_devs) % n_devs
+
+                @pl.when(jnp.logical_and(stratum > 0, jnp.logical_and(asked <= n_devs - k, jnp.logical_not(is_worker(source, n_devs)))))
+                def _():
+                    pl.semaphore_signal(go, inc=1, device_id={"shard": source}, device_id_type=pl.DeviceIdType.MESH)
+
+                turn = (asked + me % k) // k
+
+                @pl.when(jnp.logical_and(jnp.logical_and(turn >= free_turns, turn < workers), (asked + me % k) % k == 0))
+                def _():
+                    send(*block_copy(turn))
+
             for s in range(SLOTS):
                 if s == leave_slot and not ends:
                     @pl.when(stratum > 0)
@@ -271,6 +295,7 @@
                 pltpu.VMEM((k, items, rank), jnp.float32),
                 pltpu.VMEM((k, items, rank), jnp.bfloat16),
                 pltpu.VMEM((k, users, rank), jnp.float32),
+                pltpu.SemaphoreType.REGULAR,
                 dma((workers,)),
                 dma((n_devs,)),
                 dma((2,)),

time: 806 us -> 828 us (1.027)
  Pallas kernels: 795 us -> 816 us
    pallas_call x1, Pallas kernels: 795 us -> 816 us  [local(): pl.pallas_call(functools.partial(kernel, n_devs, EPOCHS * n_devs, step_si...]
where the time goes in v2:
time: 828 us
  Pallas kernels  816 us (99%)
    pallas_call x1, Pallas kernels, local(): pl.pallas_call(functools.partial(kernel, n_devs, EPOCHS * n_devs, step_si...  816 us

profile of v2, /device:TPU:39, one launch (start us, length us, event | category | flops | bytes accessed | tf_op | source)
XLA Modules:
  0.0 827.7 jit_solution(14286892158511213783)
XLA Ops:
  0.6 1.6 copy.6.item_init
  2.3 5.9 compare_select_fusion.ratings
  8.1 816.4 %strata.1 = (f32[64,192]{1,0:T(8,128)}, f32[128,192]{1,0:T(8,128)}) custom-call(f32[64,16384]{1,0:T(8,128)} %compare_select_fusion.ratings, f32[64,192]{1,0:T(8,128)} %user_init.1, f32[128,192]{1,0:T(8,128)} %copy.6.item_init), custom_call_target="tpu_custom_call" | custom-call | tf_op jit(solution)/shard_map/strata/pallas_call | solution.py:277
  824.5 1.6 copy.7
  826.2 1.5 copy.9

commit v3 on v1

--- a/solution.py
+++ b/solution.py
@@ -32,16 +32,16 @@
     odd = y % 2
     x = place % 4
     x = x + odd * (3 - 2 * x)
-    return ((plane * 4 + y) * 4 + x) * 2 + 1
+    return ((x * 4 + y) * 4 + plane) * 2 + 1
 
 
 def worker_of(dev, n_devs):
     if n_devs != 128:
         return dev // ITEM_BLOCKS
     chip = dev // 2
-    plane = (chip // 16) % 2
+    plane = chip % 2
     y = (chip // 4) % 4
-    x = chip % 4
+    x = chip // 16
     place = y * 4 + x + (y % 2) * (3 - 2 * x)
     return place + plane * (31 - 2 * place)
 
@@ -49,7 +49,7 @@
 def is_worker(dev, n_devs):
     if n_devs != 128:
         return dev % ITEM_BLOCKS == 0
-    return jnp.logical_and(dev % 2 == 1, dev < 64)
+    return jnp.logical_and(dev % 2 == 1, dev % 8 < 4)
 
 
 def kernel(n_devs, strata, step_size, weight_decay, ratings, user_init, item_init, user_out, item_out, rated, turned,

time: 806 us -> 870 us (1.079)
  Pallas kernels: 795 us -> 856 us
    pallas_call x1, Pallas kernels: 795 us -> 856 us  [local(): pl.pallas_call(functools.partial(kernel, n_devs, EPOCHS * n_devs, step_si...]
where the time goes in v3:
time: 870 us; the launch traced here: 867 us
  Pallas kernels  856 us (98%)
    pallas_call x1, Pallas kernels, local(): pl.pallas_call(functools.partial(kernel, n_devs, EPOCHS * n_devs, step_si...  856 us

profile of v3, /device:TPU:39, one launch (start us, length us, event | category | flops | bytes accessed | tf_op | source)
XLA Modules:
  0.0 866.9 jit_solution(8343635789347170215)
XLA Ops:
  0.6 1.6 copy.6.item_init
  2.3 5.9 compare_select_fusion.ratings
  8.1 855.6 %strata.1 = (f32[64,192]{1,0:T(8,128)}, f32[128,192]{1,0:T(8,128)}) custom-call(f32[64,16384]{1,0:T(8,128)} %compare_select_fusion.ratings, f32[64,192]{1,0:T(8,128)} %user_init.1, f32[128,192]{1,0:T(8,128)} %copy.6.item_init), custom_call_target="tpu_custom_call" | custom-call | tf_op jit(solution)/shard_map/strata/pallas_call | solution.py:253
  863.8 1.6 copy.7
  865.4 1.5 copy.9

commit v4 on v1

--- a/solution.py
+++ b/solution.py
@@ -32,14 +32,14 @@
     odd = y % 2
     x = place % 4
     x = x + odd * (3 - 2 * x)
-    return ((plane * 4 + y) * 4 + x) * 2 + 1
+    return ((plane * 8 + y) * 4 + x) * 2 + 1
 
 
 def worker_of(dev, n_devs):
     if n_devs != 128:
         return dev // ITEM_BLOCKS
     chip = dev // 2
-    plane = (chip // 16) % 2
+    plane = (chip // 32) % 2
     y = (chip // 4) % 4
     x = chip % 4
     place = y * 4 + x + (y % 2) * (3 - 2 * x)
@@ -49,17 +49,22 @@
 def is_worker(dev, n_devs):
     if n_devs != 128:
         return dev % ITEM_BLOCKS == 0
-    return jnp.logical_and(dev % 2 == 1, dev < 64)
+    return jnp.logical_and(dev % 2 == 1, (dev // 32) % 2 == 0)
+
+
+def partner(dev):
+    return dev + 1 - 2 * (dev % 2)
 
 
 def kernel(n_devs, strata, step_size, weight_decay, ratings, user_init, item_init, user_out, item_out, rated, turned,
            arriving, handed, handed_bf, leaving, user, user_bf, item, item_bf, user_start,
-           block_send, block_recv, start_send, user_recv, item_recv, hop_send, hop_recv, end_send, end_recv):
+           relay_send, block_send, block_recv, start_send, user_recv, item_recv, hop_send, hop_recv, end_send, end_recv):
     k = ITEM_BLOCKS
     workers = n_devs // k
     items = item_init.shape[0]
     me = lax.axis_index("shard")
     last = k - 1
+    other = partner(me)
 
     def remote(src, dst, send, recv, dev):
         return pltpu.make_async_remote_copy(
@@ -89,16 +94,56 @@
     send(*user_copy)
     send(*item_copy)
 
+    def columns_of(dev, turn):
+        worker = (dev // k + turn) % workers
+        return worker_device(worker, n_devs), pl.ds(pl.multiple_of(worker * (k * items), 128), k * items)
+
     def block_copy(turn):
-        worker = (me // k + turn) % workers
-        columns = pl.ds(pl.multiple_of(worker * (k * items), 128), k * items)
-        return ratings.at[:, columns], rated.at[me], block_send.at[turn], block_recv.at[me], worker_device(worker, n_devs)
-
-    @pl.loop(0, workers)
-    def _(turn):
-        send(*block_copy(turn))
-
-    @pl.when(is_worker(me, n_devs))
+        to, columns = columns_of(me, turn)
+        return remote(ratings.at[:, columns], rated.at[me], block_send.at[turn], block_recv.at[me], to)
+
+    def aside_copy(turn):
+        _, columns = columns_of(me, turn)
+        return remote(ratings.at[:, columns], rated.at[turn], block_send.at[turn], block_recv.at[turn], other)
+
+    def relay_copy(turn):
+        to, _ = columns_of(other, turn)
+        return remote(rated.at[turn], rated.at[other], relay_send.at[turn], block_recv.at[other], to)
+
+    def own_columns():
+        return ratings.at[:, pl.ds(pl.multiple_of(worker_of(me, n_devs) * (k * items), 128), k * items)]
+
+    working = is_worker(me, n_devs)
+    relaying = is_worker(other, n_devs)
+
+    @pl.when(working)
+    def _():
+        pltpu.make_async_copy(own_columns(), rated.at[me], block_recv.at[me]).start()
+
+        @pl.loop(0, workers)
+        def _(turn):
+            to, _ = columns_of(me, turn)
+
+            @pl.when(to != me)
+            def _():
+                aside_copy(turn).start()
+
+    @pl.when(jnp.logical_not(working))
+    def _():
+        @pl.loop(0, workers)
+        def _(turn):
+            @pl.when(relaying)
+            def _():
+                to, _ = columns_of(other, turn)
+
+                @pl.when(to != other)
+                def _():
+                    arrival(ratings.at[:, pl.ds(0, k * items)], rated.at[turn], block_recv.at[turn]).wait()
+                    relay_copy(turn).start()
+
+            block_copy(turn).start()
+
+    @pl.when(working)
     def _():
         mine = worker_of(me, n_devs)
         first = mine * k
@@ -230,7 +275,25 @@
 
     @pl.loop(0, workers)
     def _(turn):
-        wait_sent(*block_copy(turn))
+        @pl.when(working)
+        def _():
+            to, _ = columns_of(me, turn)
+
+            @pl.when(to != me)
+            def _():
+                aside_copy(turn).wait_send()
+
+        @pl.when(jnp.logical_not(working))
+        def _():
+            block_copy(turn).wait_send()
+
+            @pl.when(relaying)
+            def _():
+                to, _ = columns_of(other, turn)
+
+                @pl.when(to != other)
+                def _():
+                    relay_copy(turn).wait_send()
 
     arrival(user_init, user_out, end_recv.at[0]).wait()
     arrival(item_init, item_out, end_recv.at[1]).wait()
@@ -272,6 +335,7 @@
                 pltpu.VMEM((k, items, rank), jnp.bfloat16),
                 pltpu.VMEM((k, users, rank), jnp.float32),
                 dma((workers,)),
+                dma((workers,)),
                 dma((n_devs,)),
                 dma((2,)),
                 dma((k,)),

time: 806 us -> 812 us (level)
  no operation moved by 1% of the time
where the time goes in v4:
time: 812 us
  Pallas kernels  800 us (99%)
    pallas_call x1, Pallas kernels, local(): pl.pallas_call(functools.partial(kernel, n_devs, EPOCHS * n_devs, step_si...  800 us

profile of v4, /device:TPU:39, one launch (start us, length us, event | category | flops | bytes accessed | tf_op | source)
XLA Modules:
  0.0 811.6 jit_solution(1993917680394735959)
XLA Ops:
  0.6 1.6 copy.6.item_init
  2.3 5.9 compare_select_fusion.ratings
  8.1 800.4 %strata.1 = (f32[64,192]{1,0:T(8,128)}, f32[128,192]{1,0:T(8,128)}) custom-call(f32[64,16384]{1,0:T(8,128)} %compare_select_fusion.ratings, f32[64,192]{1,0:T(8,128)} %user_init.1, f32[128,192]{1,0:T(8,128)} %copy.6.item_init), custom_call_target="tpu_custom_call" | custom-call | tf_op jit(solution)/shard_map/strata/pallas_call | solution.py:316
  808.5 1.6 copy.7
  810.1 1.5 copy.9

commit v5 on v1

--- a/solution.py
+++ b/solution.py
@@ -12,6 +12,7 @@
 EPOCHS = 2
 ITEM_BLOCKS = 4
 SLOTS = 9
+SOON = 2
 HALF_STEPS = 2 * STRATUM_STEPS
 LEAD = SLOTS - HALF_STEPS + 1
 
@@ -94,11 +95,23 @@
         columns = pl.ds(pl.multiple_of(worker * (k * items), 128), k * items)
         return ratings.at[:, columns], rated.at[me], block_send.at[turn], block_recv.at[me], worker_device(worker, n_devs)
 
-    @pl.loop(0, workers)
+    working = is_worker(me, n_devs)
+
+    @pl.loop(0, SOON)
     def _(turn):
         send(*block_copy(turn))
 
-    @pl.when(is_worker(me, n_devs))
+    @pl.when(jnp.logical_not(working))
+    def _():
+        wait_sent(*user_copy)
+        wait_sent(*item_copy)
+        wait_sent(*block_copy(0))
+
+        @pl.loop(SOON, workers)
+        def _(turn):
+            send(*block_copy(turn))
+
+    @pl.when(working)
     def _():
         mine = worker_of(me, n_devs)
         first = mine * k
@@ -198,6 +211,11 @@
                         hop(stratum - 1).wait_send()
 
                     hop(stratum).start()
+
+                    @pl.when(stratum + SOON < workers)
+                    def _():
+                        send(*block_copy(stratum + SOON))
+
                 slot(work_of(s, stratum, ends))
 
         for s in range(-LEAD * last, 0):
@@ -225,10 +243,13 @@
             for copy in end_copies(c):
                 wait_sent(*copy)
 
-    wait_sent(*user_copy)
-    wait_sent(*item_copy)
-
-    @pl.loop(0, workers)
+    @pl.when(working)
+    def _():
+        wait_sent(*user_copy)
+        wait_sent(*item_copy)
+        wait_sent(*block_copy(0))
+
+    @pl.loop(1, workers)
     def _(turn):
         wait_sent(*block_copy(turn))
 

time: 806 us -> 818 us (1.015)
  Pallas kernels: 795 us -> 806 us
    pallas_call x1, Pallas kernels: 795 us -> 806 us  [local(): pl.pallas_call(functools.partial(kernel, n_devs, EPOCHS * n_devs, step_si...]
where the time goes in v5:
time: 818 us; the launch traced here: 817 us
  Pallas kernels  806 us (99%)
    pallas_call x1, Pallas kernels, local(): pl.pallas_call(functools.partial(kernel, n_devs, EPOCHS * n_devs, step_si...  806 us

profile of v5, /device:TPU:39, one launch (start us, length us, event | category | flops | bytes accessed | tf_op | source)
XLA Modules:
  0.0 817.3 jit_solution(3343179057633844926)
XLA Ops:
  0.6 1.6 copy.6.item_init
  2.3 5.9 compare_select_fusion.ratings
  8.1 806.0 %strata.1 = (f32[64,192]{1,0:T(8,128)}, f32[128,192]{1,0:T(8,128)}) custom-call(f32[64,16384]{1,0:T(8,128)} %compare_select_fusion.ratings, f32[64,192]{1,0:T(8,128)} %user_init.1, f32[128,192]{1,0:T(8,128)} %copy.6.item_init), custom_call_target="tpu_custom_call" | custom-call | tf_op jit(solution)/shard_map/strata/pallas_call | solution.py:274
  814.2 1.6 copy.7
  815.8 1.5 copy.9

commit v6 on v1

--- a/solution.py
+++ b/solution.py
@@ -12,6 +12,8 @@
 EPOCHS = 2
 ITEM_BLOCKS = 4
 SLOTS = 9
+AHEAD = 12
+SOON = 2
 HALF_STEPS = 2 * STRATUM_STEPS
 LEAD = SLOTS - HALF_STEPS + 1
 
@@ -25,7 +27,7 @@
 
 def worker_device(worker, n_devs):
     if n_devs != 128:
-        return worker * ITEM_BLOCKS
+        return worker
     plane = worker // 16
     place = worker + plane * (31 - 2 * worker)
     y = place // 4
@@ -37,7 +39,7 @@
 
 def worker_of(dev, n_devs):
     if n_devs != 128:
-        return dev // ITEM_BLOCKS
+        return dev
     chip = dev // 2
     plane = (chip // 16) % 2
     y = (chip // 4) % 4
@@ -48,13 +50,22 @@
 
 def is_worker(dev, n_devs):
     if n_devs != 128:
-        return dev % ITEM_BLOCKS == 0
+        return dev < n_devs // ITEM_BLOCKS
     return jnp.logical_and(dev % 2 == 1, dev < 64)
+
+
+def is_low(dev, n_devs):
+    return dev < n_devs // 2
+
+
+def mirror(dev, n_devs):
+    quarter = n_devs // 4
+    return dev + quarter * (3 - 2 * (dev // quarter))
 
 
 def kernel(n_devs, strata, step_size, weight_decay, ratings, user_init, item_init, user_out, item_out, rated, turned,
            arriving, handed, handed_bf, leaving, user, user_bf, item, item_bf, user_start,
-           block_send, block_recv, start_send, user_recv, item_recv, hop_send, hop_recv, end_send, end_recv):
+           go, more_own, more_relayed, relay_send, block_send, block_recv, start_send, user_recv, item_recv, hop_send, hop_recv, end_send, end_recv):
     k = ITEM_BLOCKS
     workers = n_devs // k
     items = item_init.shape[0]
@@ -89,16 +100,76 @@
     send(*user_copy)
     send(*item_copy)
 
+    def columns_of(dev, turn):
+        worker = (dev // k + turn) % workers
+        return worker_device(worker, n_devs), pl.ds(pl.multiple_of(worker * (k * items), 128), k * items)
+
     def block_copy(turn):
-        worker = (me // k + turn) % workers
-        columns = pl.ds(pl.multiple_of(worker * (k * items), 128), k * items)
-        return ratings.at[:, columns], rated.at[me], block_send.at[turn], block_recv.at[me], worker_device(worker, n_devs)
-
-    @pl.loop(0, workers)
+        to, columns = columns_of(me, turn)
+        return ratings.at[:, columns], rated.at[me], block_send.at[turn], block_recv.at[me], to
+
+    low = is_low(me, n_devs)
+    across = mirror(me, n_devs)
+
+    def up_copy(turn):
+        _, columns = columns_of(me, turn)
+        return remote(ratings.at[:, columns], rated.at[turn], block_send.at[turn], block_recv.at[turn], across)
+
+    def relay_copy(turn):
+        to, _ = columns_of(across, turn)
+        return remote(rated.at[turn], rated.at[across], relay_send.at[turn], block_recv.at[across], to)
+
+    def block_out(turn):
+        return remote(*block_copy(turn))
+
+    @pl.loop(0, SOON)
     def _(turn):
         send(*block_copy(turn))
 
-    @pl.when(is_worker(me, n_devs))
+    def send_up():
+        @pl.loop(SOON, workers)
+        def _(turn):
+            to, columns = columns_of(me, turn)
+
+            @pl.when(to != me)
+            def _():
+                up_copy(turn).start()
+
+            @pl.when(to == me)
+            def _():
+                pltpu.make_async_copy(ratings.at[:, columns], rated.at[me], block_recv.at[me]).start()
+
+    working = is_worker(me, n_devs)
+
+    @pl.when(low)
+    def _():
+        send_up()
+
+    @pl.when(jnp.logical_not(low))
+    def _():
+        pl.semaphore_wait(go, 1)
+
+        @pl.loop(SOON, workers)
+        def _(turn):
+            to, _ = columns_of(across, turn)
+            relays = to != across
+
+            @pl.when(turn * k - me % k > AHEAD)
+            def _():
+                pl.semaphore_wait(more_own, 1)
+
+                @pl.when(relays)
+                def _():
+                    pl.semaphore_wait(more_relayed, 1)
+
+            block_out(turn).start()
+
+            @pl.when(relays)
+            def _():
+                arrival(ratings.at[:, pl.ds(0, k * items)], rated.at[turn], block_recv.at[turn]).wait()
+                relay_copy(turn).start()
+
+    @pl.when(working)
     def _():
         mine = worker_of(me, n_devs)
         first = mine * k
@@ -115,6 +186,11 @@
             arrival(user_init, user_start.at[c], user_recv.at[c]).wait()
             arrival(item_init, item.at[c], item_recv.at[c]).wait()
             wait_block(first + c)
+        for c in range(k):
+            @pl.when(jnp.logical_not(is_low(first + c, n_devs)))
+            def _():
+                pl.semaphore_signal(go, inc=1, device_id={"shard": first + c}, device_id_type=pl.DeviceIdType.MESH)
+
         for c in range(k):
             if c == 0:
                 arriving[0] = user_start[0]
@@ -191,6 +267,19 @@
             def _():
                 wait_block((first - stratum + n_devs) % n_devs)
 
+            if not ends:
+                asked = (first - stratum - AHEAD + 2 * n_devs) % n_devs
+
+                @pl.when(jnp.logical_and(stratum > 0, jnp.logical_and(stratum + AHEAD <= n_devs - k, asked != me)))
+                def _():
+                    @pl.when(is_low(asked, n_devs))
+                    def _():
+                        pl.semaphore_signal(more_relayed, inc=1, device_id={"shard": mirror(asked, n_devs)}, device_id_type=pl.DeviceIdType.MESH)
+
+                    @pl.when(jnp.logical_not(is_low(asked, n_devs)))
+                    def _():
+                        pl.semaphore_signal(more_own, inc=1, device_id={"shard": asked}, device_id_type=pl.DeviceIdType.MESH)
+
             for s in range(SLOTS):
                 if s == leave_slot and not ends:
                     @pl.when(stratum > 0)
@@ -228,9 +317,30 @@
     wait_sent(*user_copy)
     wait_sent(*item_copy)
 
-    @pl.loop(0, workers)
+    @pl.loop(0, SOON)
     def _(turn):
         wait_sent(*block_copy(turn))
+
+    @pl.when(low)
+    def _():
+        @pl.loop(SOON, workers)
+        def _(turn):
+            to, _ = columns_of(me, turn)
+
+            @pl.when(to != me)
+            def _():
+                up_copy(turn).wait_send()
+
+    @pl.when(jnp.logical_not(low))
+    def _():
+        @pl.loop(SOON, workers)
+        def _(turn):
+            block_out(turn).wait_send()
+            to, _ = columns_of(across, turn)
+
+            @pl.when(to != across)
+            def _():
+                relay_copy(turn).wait_send()
 
     arrival(user_init, user_out, end_recv.at[0]).wait()
     arrival(item_init, item_out, end_recv.at[1]).wait()
@@ -271,6 +381,10 @@
                 pltpu.VMEM((k, items, rank), jnp.float32),
                 pltpu.VMEM((k, items, rank), jnp.bfloat16),
                 pltpu.VMEM((k, users, rank), jnp.float32),
+                pltpu.SemaphoreType.REGULAR,
+                pltpu.SemaphoreType.REGULAR,
+                pltpu.SemaphoreType.REGULAR,
+                dma((workers,)),
                 dma((workers,)),
                 dma((n_devs,)),
                 dma((2,)),

time: 806 us -> 771 us (0.957)
  Pallas kernels: 795 us -> 759 us
    pallas_call x1, Pallas kernels: 795 us -> 759 us  [local(): pl.pallas_call(functools.partial(kernel, n_devs, EPOCHS * n_devs, step_si...]
where the time goes in v6:
time: 771 us
  Pallas kernels  759 us (98%)
    pallas_call x1, Pallas kernels, local(): pl.pallas_call(functools.partial(kernel, n_devs, EPOCHS * n_devs, step_si...  759 us

profile of v6, /device:TPU:39, one launch (start us, length us, event | category | flops | bytes accessed | tf_op | source)
XLA Modules:
  0.0 770.6 jit_solution(7102638407542517430)
XLA Ops:
  0.6 1.6 copy.6.item_init
  2.3 5.9 compare_select_fusion.ratings
  8.1 759.4 %strata.1 = (f32[64,192]{1,0:T(8,128)}, f32[128,192]{1,0:T(8,128)}) custom-call(f32[64,16384]{1,0:T(8,128)} %compare_select_fusion.ratings, f32[64,192]{1,0:T(8,128)} %user_init.1, f32[128,192]{1,0:T(8,128)} %copy.6.item_init), custom_call_target="tpu_custom_call" | custom-call | tf_op jit(solution)/shard_map/strata/pallas_call | solution.py:363
  767.5 1.6 copy.7
  769.1 1.5 copy.9

commit v7 on v6

--- a/solution.py
+++ b/solution.py
@@ -13,6 +13,9 @@
 ITEM_BLOCKS = 4
 SLOTS = 9
 AHEAD = 12
+PHASES = (0.0, 0.5, 0.9)
+SHIFTS = (0.0,) * ITEM_BLOCKS
+ORDER = (3, 2, 1, 0)
 SOON = 2
 HALF_STEPS = 2 * STRATUM_STEPS
 LEAD = SLOTS - HALF_STEPS + 1
@@ -196,21 +199,21 @@
                 arriving[0] = user_start[0]
             else:
                 handed[c - 1] = user_start[c]
-                handed_bf[c - 1] = user_start[c].astype(jnp.bfloat16)
-            item_bf[c] = item[c].astype(jnp.bfloat16)
-
-        def slot(work):
-            first_product, residual = {}, {}
-            for c, half, stratum in work:
+
+        def steps_of(c, half, stratum, send_user):
+            kept = {}
+
+            def predict():
                 if half == 0:
-                    lhs = arriving[stratum % n_devs].astype(jnp.bfloat16) if c == 0 else handed_bf[c - 1]
+                    lhs = arriving[stratum % n_devs] if c == 0 else handed[c - 1]
                 else:
-                    lhs = user_bf[c]
+                    lhs = user[c] if half < HALF_STEPS - 1 else (handed[c] if c < last else leaving[stratum % 2])
                 if half % 2 == 0:
-                    first_product[c] = dot(lhs, item_bf[c], ROW_BY_ROW)
+                    kept["predicted"] = dot(lhs, item[c], ROW_BY_ROW)
                 else:
-                    first_product[c] = dot(item_bf[c], lhs, ROW_BY_ROW)
-            for c, half, stratum in work:
+                    kept["predicted"] = dot(item[c], lhs, ROW_BY_ROW)
+
+            def descend():
                 if half % 2 == 0:
                     block = (first + c - stratum + 2 * n_devs) % n_devs
                     known = rated[block, :, c * items : (c + 1) * items]
@@ -218,8 +221,10 @@
                         turned[c] = known.T
                 else:
                     known = turned[c]
-                residual[c] = jnp.where(known != known, 0.0, first_product[c] - known).astype(jnp.bfloat16)
-            for c, half, stratum in work:
+                residual = jnp.where(known != known, 0.0, kept["predicted"] - known)
+                kept["grad"] = dot(residual, item[c] if half % 2 == 0 else (user[c] if half < HALF_STEPS - 1 else (handed[c] if c < last else leaving[stratum % 2])), PLAIN)
+
+            def update():
                 if half % 2 == 0:
                     if half > 0:
                         old = user[c]
@@ -227,23 +232,30 @@
                         old = arriving[stratum % n_devs]
                     else:
                         old = handed[c - 1]
-                    grad = dot(residual[c], item_bf[c], PLAIN)
-                    new = old - step_size * (grad + weight_decay * old)
-                    new_bf = new.astype(jnp.bfloat16)
-                    user_bf[c] = new_bf
-                    if half < HALF_STEPS - 2:
-                        user[c] = new
-                    elif c < last:
-                        handed[c] = new
-                        handed_bf[c] = new_bf
-                    else:
-                        leaving[stratum % 2] = new
                 else:
                     old = item[c]
-                    grad = dot(residual[c], user_bf[c], PLAIN)
-                    new = old - step_size * (grad + weight_decay * old)
+                new = old - step_size * (kept["grad"] + weight_decay * old)
+                if half % 2 == 1:
                     item[c] = new
-                    item_bf[c] = new.astype(jnp.bfloat16)
+                    return
+                if half < HALF_STEPS - 2:
+                    user[c] = new
+                elif c < last:
+                    handed[c] = new
+                else:
+                    leaving[stratum % 2] = new
+                    if send_user is not None:
+                        send_user(stratum)
+
+            return predict, descend, update
+
+        def run(slots, send_user=None):
+            steps = []
+            for s, c, half, stratum in slots:
+                for phase, step in zip(PHASES, steps_of(c, half, stratum, send_user)):
+                    steps.append((s + phase + SHIFTS[c], ORDER[c], step))
+            for _, _, step in sorted(steps, key=lambda step: step[:2]):
+                step()
 
         def work_of(s, stratum, first_only=False):
             work = []
@@ -252,12 +264,15 @@
                 if place < 0 or (first_only and place >= SLOTS):
                     continue
                 if place % SLOTS < HALF_STEPS:
-                    work.append((c, place % SLOTS, stratum + place // SLOTS))
+                    work.append((s, c, place % SLOTS, stratum + place // SLOTS))
             return work
 
-        leave_slot = (HALF_STEPS - 1 - LEAD * last) % SLOTS
+        sent_next = LEAD * last > HALF_STEPS - 2
 
         def stratum_body(stratum, ends):
+            if sent_next and not ends:
+                send_user(stratum)
+
             @pl.when(stratum > 0)
             def _():
                 slot_in = stratum % n_devs
@@ -280,17 +295,16 @@
                     def _():
                         pl.semaphore_signal(more_own, inc=1, device_id={"shard": asked}, device_id_type=pl.DeviceIdType.MESH)
 
-            for s in range(SLOTS):
-                if s == leave_slot and not ends:
-                    @pl.when(stratum > 0)
-                    def _():
-                        hop(stratum - 1).wait_send()
-
-                    hop(stratum).start()
-                slot(work_of(s, stratum, ends))
-
-        for s in range(-LEAD * last, 0):
-            slot(work_of(s, 0))
+            run([w for s in range(SLOTS) for w in work_of(s, stratum, ends)], None if sent_next or ends else send_user)
+
+        def send_user(stratum):
+            hop(stratum).start()
+
+            @pl.when(stratum > 0)
+            def _():
+                hop(stratum - 1).wait_send()
+
+        run([w for s in range(-LEAD * last, 0) for w in work_of(s, 0)])
 
         @pl.loop(0, strata - 1)
         def _(stratum):

time: 771 us -> 774 us (level)
  no operation moved by 1% of the time
where the time goes in v7:
time: 774 us; the launch traced here: 773 us
  Pallas kernels  762 us (98%)
    pallas_call x1, Pallas kernels, local(): pl.pallas_call(functools.partial(kernel, n_devs, EPOCHS * n_devs, step_si...  762 us

profile of v7, /device:TPU:39, one launch (start us, length us, event | category | flops | bytes accessed | tf_op | source)
XLA Modules:
  0.0 773.4 jit_solution(13426874117838010107)
XLA Ops:
  0.6 1.6 copy.6.item_init
  2.3 5.9 compare_select_fusion.ratings
  8.1 762.1 %strata.1 = (f32[64,192]{1,0:T(8,128)}, f32[128,192]{1,0:T(8,128)}) custom-call(f32[64,16384]{1,0:T(8,128)} %compare_select_fusion.ratings, f32[64,192]{1,0:T(8,128)} %user_init.1, f32[128,192]{1,0:T(8,128)} %copy.6.item_init), custom_call_target="tpu_custom_call" | custom-call | tf_op jit(solution)/shard_map/strata/pallas_call | solution.py:377
  770.3 1.6 copy.7
  771.9 1.5 copy.9

commit v8 on v7

--- a/solution.py
+++ b/solution.py
@@ -199,19 +199,21 @@
                 arriving[0] = user_start[0]
             else:
                 handed[c - 1] = user_start[c]
+                handed_bf[c - 1] = user_start[c].astype(jnp.bfloat16)
+            item_bf[c] = item[c].astype(jnp.bfloat16)
 
         def steps_of(c, half, stratum, send_user):
             kept = {}
 
             def predict():
                 if half == 0:
-                    lhs = arriving[stratum % n_devs] if c == 0 else handed[c - 1]
+                    lhs = arriving[stratum % n_devs].astype(jnp.bfloat16) if c == 0 else handed_bf[c - 1]
                 else:
-                    lhs = user[c] if half < HALF_STEPS - 1 else (handed[c] if c < last else leaving[stratum % 2])
+                    lhs = user_bf[c]
                 if half % 2 == 0:
-                    kept["predicted"] = dot(lhs, item[c], ROW_BY_ROW)
+                    kept["predicted"] = dot(lhs, item_bf[c], ROW_BY_ROW)
                 else:
-                    kept["predicted"] = dot(item[c], lhs, ROW_BY_ROW)
+                    kept["predicted"] = dot(item_bf[c], lhs, ROW_BY_ROW)
 
             def descend():
                 if half % 2 == 0:
@@ -221,8 +223,8 @@
                         turned[c] = known.T
                 else:
                     known = turned[c]
-                residual = jnp.where(known != known, 0.0, kept["predicted"] - known)
-                kept["grad"] = dot(residual, item[c] if half % 2 == 0 else (user[c] if half < HALF_STEPS - 1 else (handed[c] if c < last else leaving[stratum % 2])), PLAIN)
+                residual = jnp.where(known != known, 0.0, kept["predicted"] - known).astype(jnp.bfloat16)
+                kept["grad"] = dot(residual, item_bf[c] if half % 2 == 0 else user_bf[c], PLAIN)
 
             def update():
                 if half % 2 == 0:
@@ -234,14 +236,18 @@
                         old = handed[c - 1]
                 else:
                     old = item[c]
-                new = old - step_size * (kept["grad"] + weight_decay * old)
+                new = old * (1 - step_size * weight_decay) - step_size * kept["grad"]
+                new_bf = new.astype(jnp.bfloat16)
                 if half % 2 == 1:
                     item[c] = new
+                    item_bf[c] = new_bf
                     return
+                user_bf[c] = new_bf
                 if half < HALF_STEPS - 2:
                     user[c] = new
                 elif c < last:
                     handed[c] = new
+                    handed_bf[c] = new_bf
                 else:
                     leaving[stratum % 2] = new
                     if send_user is not None:

time: 774 us -> 763 us (0.986)
  Pallas kernels: 762 us -> 751 us
    pallas_call x1, Pallas kernels: 762 us -> 751 us  [local(): pl.pallas_call(functools.partial(kernel, n_devs, EPOCHS * n_devs, step_si...]
where the time goes in v8:
time: 763 us
  Pallas kernels  751 us (98%)
    pallas_call x1, Pallas kernels, local(): pl.pallas_call(functools.partial(kernel, n_devs, EPOCHS * n_devs, step_si...  751 us

profile of v8, /device:TPU:39, one launch (start us, length us, event | category | flops | bytes accessed | tf_op | source)
XLA Modules:
  0.0 762.6 jit_solution(5635657054850996101)
XLA Ops:
  0.6 1.6 copy.6.item_init
  2.3 5.9 compare_select_fusion.ratings
  8.1 751.3 %strata.1 = (f32[64,192]{1,0:T(8,128)}, f32[128,192]{1,0:T(8,128)}) custom-call(f32[64,16384]{1,0:T(8,128)} %compare_select_fusion.ratings, f32[64,192]{1,0:T(8,128)} %user_init.1, f32[128,192]{1,0:T(8,128)} %copy.6.item_init), custom_call_target="tpu_custom_call" | custom-call | tf_op jit(solution)/shard_map/strata/pallas_call | solution.py:383
  759.4 1.6 copy.7
  761.1 1.5 copy.9

commit v9 on v8

--- a/solution.py
+++ b/solution.py
@@ -13,9 +13,6 @@
 ITEM_BLOCKS = 4
 SLOTS = 9
 AHEAD = 12
-PHASES = (0.0, 0.5, 0.9)
-SHIFTS = (0.0,) * ITEM_BLOCKS
-ORDER = (3, 2, 1, 0)
 SOON = 2
 HALF_STEPS = 2 * STRATUM_STEPS
 LEAD = SLOTS - HALF_STEPS + 1
@@ -66,12 +63,15 @@
     return dev + quarter * (3 - 2 * (dev // quarter))
 
 
-def kernel(n_devs, strata, step_size, weight_decay, ratings, user_init, item_init, user_out, item_out, rated, turned,
-           arriving, handed, handed_bf, leaving, user, user_bf, item, item_bf, user_start,
-           go, more_own, more_relayed, relay_send, block_send, block_recv, start_send, user_recv, item_recv, hop_send, hop_recv, end_send, end_recv):
+def kernel(n_devs, strata, step_size, weight_decay, ratings, observed, user_init, item_init, user_out, item_out,
+           masked, seen, rated, turned,
+           arriving, handed, handed_bf, leaving, user, user_bf, item, item_bf, user_start, item_start,
+           ratings_here, seen_here, go, more_own, more_relayed, relay_send, first_send, first_recv, block_send, block_recv,
+           start_send, user_recv, item_recv, hop_send, hop_recv, end_send, end_recv):
     k = ITEM_BLOCKS
     workers = n_devs // k
-    items = item_init.shape[0]
+    items = item_init.shape[1]
+    wide = k * items
     me = lax.axis_index("shard")
     last = k - 1
 
@@ -97,26 +97,58 @@
         def _():
             remote(src, dst, send_sem, recv_sem, dev).wait_send()
 
+    low = is_low(me, n_devs)
+    across = mirror(me, n_devs)
+    pair_here = me % k
     home = worker_device(me // k, n_devs)
-    user_copy = (user_init, user_start.at[me % k], start_send.at[0], user_recv.at[me % k], home)
-    item_copy = (item_init, item.at[me % k], start_send.at[1], item_recv.at[me % k], home)
+
+    def columns_of(dev, turn):
+        worker = (dev // k + turn) % workers
+        return worker_device(worker, n_devs), pl.ds(pl.multiple_of(worker * wide, 128), wide)
+
+    def fetch(turn):
+        _, columns = columns_of(me, turn)
+        return (
+            pltpu.make_async_copy(ratings.at[:, columns], masked.at[:, columns], ratings_here.at[turn]),
+            pltpu.make_async_copy(observed.at[:, columns], seen.at[:, columns], seen_here.at[turn]),
+        )
+
+    def mask(turn):
+        for copy in fetch(turn):
+            copy.wait()
+        _, columns = columns_of(me, turn)
+        masked[:, columns] = jnp.where(seen[:, columns] != 0, masked[:, columns], jnp.nan)
+
+    for copy in fetch(0):
+        copy.start()
+    user_copy = (user_init, user_start.at[pair_here], start_send.at[0], user_recv.at[pair_here], home)
+    item_copy = (item_init, item_start.at[pair_here], start_send.at[1], item_recv.at[pair_here], home)
     send(*user_copy)
     send(*item_copy)
 
-    def columns_of(dev, turn):
-        worker = (dev // k + turn) % workers
-        return worker_device(worker, n_devs), pl.ds(pl.multiple_of(worker * (k * items), 128), k * items)
+    @pl.loop(1, workers)
+    def _(turn):
+        for copy in fetch(turn):
+            copy.start()
+
+    def part_copy(ahead):
+        pair = (pair_here + ahead) % k
+        here = pl.ds(pl.multiple_of((me // k) * wide + pair * items, 128), items)
+        there = pl.ds(pl.multiple_of(pair * items, 128), items)
+        sent, received = (first_send, first_recv.at[pair]) if ahead == 0 else (block_send.at[0], block_recv.at[me])
+        return masked.at[:, here], rated.at[me, :, there], sent, received, home
+
+    mask(0)
+    for ahead in range(k):
+        send(*part_copy(ahead))
 
     def block_copy(turn):
         to, columns = columns_of(me, turn)
-        return ratings.at[:, columns], rated.at[me], block_send.at[turn], block_recv.at[me], to
-
-    low = is_low(me, n_devs)
-    across = mirror(me, n_devs)
+        return masked.at[:, columns], rated.at[me], block_send.at[turn], block_recv.at[me], to
 
     def up_copy(turn):
         _, columns = columns_of(me, turn)
-        return remote(ratings.at[:, columns], rated.at[turn], block_send.at[turn], block_recv.at[turn], across)
+        return remote(masked.at[:, columns], rated.at[turn], block_send.at[turn], block_recv.at[turn], across)
 
     def relay_copy(turn):
         to, _ = columns_of(across, turn)
@@ -125,14 +157,16 @@
     def block_out(turn):
         return remote(*block_copy(turn))
 
-    @pl.loop(0, SOON)
+    @pl.loop(1, SOON)
     def _(turn):
+        mask(turn)
         send(*block_copy(turn))
 
     def send_up():
         @pl.loop(SOON, workers)
         def _(turn):
-            to, columns = columns_of(me, turn)
+            mask(turn)
+            to, _ = columns_of(me, turn)
 
             @pl.when(to != me)
             def _():
@@ -140,7 +174,8 @@
 
             @pl.when(to == me)
             def _():
-                pltpu.make_async_copy(ratings.at[:, columns], rated.at[me], block_recv.at[me]).start()
+                source, target, _, received, _ = block_copy(turn)
+                pltpu.make_async_copy(source, target, received).start()
 
     working = is_worker(me, n_devs)
 
@@ -150,6 +185,10 @@
 
     @pl.when(jnp.logical_not(low))
     def _():
+        @pl.loop(SOON, workers)
+        def _(turn):
+            mask(turn)
+
         pl.semaphore_wait(go, 1)
 
         @pl.loop(SOON, workers)
@@ -169,7 +208,7 @@
 
             @pl.when(relays)
             def _():
-                arrival(ratings.at[:, pl.ds(0, k * items)], rated.at[turn], block_recv.at[turn]).wait()
+                arrival(rated.at[turn], rated.at[turn], block_recv.at[turn]).wait()
                 relay_copy(turn).start()
 
     @pl.when(working)
@@ -179,7 +218,7 @@
         after = worker_device((mine + 1) % workers, n_devs)
 
         def wait_block(block):
-            arrival(ratings.at[:, pl.ds(0, k * items)], rated.at[block], block_recv.at[block]).wait()
+            arrival(rated.at[block], rated.at[block], block_recv.at[block]).wait()
 
         def hop(stratum):
             slot = (stratum + 1) % n_devs
@@ -187,8 +226,9 @@
 
         for c in range(k):
             arrival(user_init, user_start.at[c], user_recv.at[c]).wait()
-            arrival(item_init, item.at[c], item_recv.at[c]).wait()
-            wait_block(first + c)
+            arrival(item_init, item_start.at[c], item_recv.at[c]).wait()
+            part = rated.at[first + c, :, c * items : (c + 1) * items]
+            arrival(part, part, first_recv.at[c]).wait()
         for c in range(k):
             @pl.when(jnp.logical_not(is_low(first + c, n_devs)))
             def _():
@@ -200,6 +240,7 @@
             else:
                 handed[c - 1] = user_start[c]
                 handed_bf[c - 1] = user_start[c].astype(jnp.bfloat16)
+            item[c] = item_start[c].T
             item_bf[c] = item[c].astype(jnp.bfloat16)
 
         def steps_of(c, half, stratum, send_user):
@@ -255,13 +296,11 @@
 
             return predict, descend, update
 
-        def run(slots, send_user=None):
-            steps = []
-            for s, c, half, stratum in slots:
-                for phase, step in zip(PHASES, steps_of(c, half, stratum, send_user)):
-                    steps.append((s + phase + SHIFTS[c], ORDER[c], step))
-            for _, _, step in sorted(steps, key=lambda step: step[:2]):
-                step()
+        def slot(work, send_user=None):
+            steps = [steps_of(c, half, stratum, send_user) for c, half, stratum in reversed(work)]
+            for step in zip(*steps):
+                for of_pair in step:
+                    of_pair()
 
         def work_of(s, stratum, first_only=False):
             work = []
@@ -270,15 +309,10 @@
                 if place < 0 or (first_only and place >= SLOTS):
                     continue
                 if place % SLOTS < HALF_STEPS:
-                    work.append((s, c, place % SLOTS, stratum + place // SLOTS))
+                    work.append((c, place % SLOTS, stratum + place // SLOTS))
             return work
 
-        sent_next = LEAD * last > HALF_STEPS - 2
-
         def stratum_body(stratum, ends):
-            if sent_next and not ends:
-                send_user(stratum)
-
             @pl.when(stratum > 0)
             def _():
                 slot_in = stratum % n_devs
@@ -301,7 +335,8 @@
                     def _():
                         pl.semaphore_signal(more_own, inc=1, device_id={"shard": asked}, device_id_type=pl.DeviceIdType.MESH)
 
-            run([w for s in range(SLOTS) for w in work_of(s, stratum, ends)], None if sent_next or ends else send_user)
+            for s in range(SLOTS):
+                slot(work_of(s, stratum, ends), None if ends else send_user)
 
         def send_user(stratum):
             hop(stratum).start()
@@ -310,7 +345,12 @@
             def _():
                 hop(stratum - 1).wait_send()
 
-        run([w for s in range(-LEAD * last, 0) for w in work_of(s, 0)])
+        for s in range(-LEAD * last, 0):
+            slot(work_of(s, 0))
+
+        for c in range(k):
+            some = rated.at[first + c, :, pl.ds(0, last * items)]
+            arrival(some, some, block_recv.at[first + c]).wait()
 
         @pl.loop(0, strata - 1)
         def _(stratum):
@@ -324,9 +364,11 @@
             block = first + c
             return (
                 (done, user_out, end_send.at[2 * c], end_recv.at[0], (block + 1) % n_devs),
-                (item.at[c], item_out, end_send.at[2 * c + 1], end_recv.at[1], block),
+                (item_start.at[c], item_out, end_send.at[2 * c + 1], end_recv.at[1], block),
             )
 
+        for c in range(k):
+            item_start[c] = item[c].T
         for c in range(k):
             for copy in end_copies(c):
                 send(*copy)
@@ -337,7 +379,14 @@
     wait_sent(*user_copy)
     wait_sent(*item_copy)
 
-    @pl.loop(0, SOON)
+    wait_sent(*part_copy(0))
+
+    @pl.when(home != me)
+    def _():
+        some = rated.at[me, :, pl.ds(0, last * items)]
+        arrival(some, some, block_send.at[0]).wait()
+
+    @pl.loop(1, SOON)
     def _(turn):
         wait_sent(*block_copy(turn))
 
@@ -375,22 +424,20 @@
     def local(ratings, observed, user_init, item_init):
         users, rank = user_init.shape
         items = item_init.shape[0]
+        wide = k * items
         step_scale = (users + items + rank) / math.sqrt(rank)
         step_size = 0.5 / step_scale
         weight_decay = 0.03 * math.sqrt(users * items / rank)
-        masked = jnp.where(observed != 0, ratings, jnp.nan)
         dma = pltpu.SemaphoreType.DMA
-        return pl.pallas_call(
+        user_new, item_new = pl.pallas_call(
             functools.partial(kernel, n_devs, EPOCHS * n_devs, step_size, weight_decay),
-            out_shape=(jax.ShapeDtypeStruct((users, rank), jnp.float32), jax.ShapeDtypeStruct((items, rank), jnp.float32)),
-            in_specs=[
-                pl.BlockSpec(memory_space=pl.ANY),
-                pl.BlockSpec(memory_space=pltpu.VMEM),
-                pl.BlockSpec(memory_space=pltpu.VMEM),
-            ],
-            out_specs=(pl.BlockSpec(memory_space=pltpu.VMEM), pl.BlockSpec(memory_space=pltpu.VMEM)),
+            out_shape=(jax.ShapeDtypeStruct((users, rank), jnp.float32), jax.ShapeDtypeStruct((rank, items), jnp.float32)),
+            in_specs=[pl.BlockSpec(memory_space=pl.ANY)] * 4,
+            out_specs=(pl.BlockSpec(memory_space=pl.ANY),) * 2,
             scratch_shapes=[
-                pltpu.VMEM((n_devs, users, k * items), jnp.float32),
+                pltpu.VMEM((users, n_devs * items), jnp.float32),
+                pltpu.VMEM((users, n_devs * items), jnp.int32),
+                pltpu.VMEM((n_devs, users, wide), jnp.float32),
                 pltpu.VMEM((k, items, users), jnp.float32),
                 pltpu.VMEM((n_devs, users, rank), jnp.float32),
                 pltpu.VMEM((k - 1, users, rank), jnp.float32),
@@ -401,10 +448,15 @@
                 pltpu.VMEM((k, items, rank), jnp.float32),
                 pltpu.VMEM((k, items, rank), jnp.bfloat16),
                 pltpu.VMEM((k, users, rank), jnp.float32),
+                pltpu.VMEM((k, rank, items), jnp.float32),
+                dma((workers,)),
+                dma((workers,)),
                 pltpu.SemaphoreType.REGULAR,
                 pltpu.SemaphoreType.REGULAR,
                 pltpu.SemaphoreType.REGULAR,
                 dma((workers,)),
+                dma,
+                dma((k,)),
                 dma((workers,)),
                 dma((n_devs,)),
                 dma((2,)),
@@ -417,6 +469,7 @@
             ],
             compiler_params=pltpu.CompilerParams(has_side_effects=True, vmem_limit_bytes=60 * 2**20),
             name="strata",
-        )(masked, user_init, item_init)
+        )(ratings, observed, user_init, item_init.T)
+        return user_new, item_new.T
 
     return jax.shard_map(local, mesh=mesh, in_specs=(row_spec,) * 4, out_specs=(row_spec, row_spec), check_vma=False)

time: 763 us -> 753 us (0.987)
  no operation moved by 1% of the time
where the time goes in v9:
time: 753 us
  Pallas kernels  749 us (99%)
    pallas_call x1, Pallas kernels, local(): pl.pallas_call(functools.partial(kernel, n_devs, EPOCHS * n_devs, step_si...  749 us

profile of v9, /device:TPU:39, one launch (start us, length us, event | category | flops | bytes accessed | tf_op | source)
XLA Modules:
  0.0 752.6 jit_solution(11099684097961818972)
XLA Ops:
  0.6 749.0 %strata.1 = (f32[64,192]{1,0:T(8,128)}, f32[192,128]{1,0:T(8,128)}) custom-call(f32[64,16384]{1,0:T(8,128)} %ratings.1, s32[64,16384]{1,0:T(8,128)} %observed.1, f32[64,192]{1,0:T(8,128)} %user_init.1, f32[192,128]{1,0:T(8,128)} %bitcast.2), custom_call_target="tpu_custom_call" | custom-call | tf_op jit(solution)/shard_map/strata/pallas_call | solution.py:432
  749.6 1.5 copy.8
  751.1 1.5 copy.9

commit v10 on v9

--- a/solution.py
+++ b/solution.py
@@ -160,6 +160,13 @@
     @pl.loop(1, SOON)
     def _(turn):
         mask(turn)
+
+    wait_sent(*user_copy)
+    wait_sent(*item_copy)
+    wait_sent(*part_copy(0))
+
+    @pl.loop(1, SOON)
+    def _(turn):
         send(*block_copy(turn))
 
     def send_up():
@@ -312,37 +319,33 @@
                     work.append((c, place % SLOTS, stratum + place // SLOTS))
             return work
 
-        def stratum_body(stratum, ends):
-            @pl.when(stratum > 0)
-            def _():
+        def ask(stratum):
+            asked = (first - stratum + 2 * n_devs) % n_devs
+
+            @pl.when(jnp.logical_and(stratum <= n_devs - k, asked != me))
+            def _():
+                @pl.when(is_low(asked, n_devs))
+                def _():
+                    pl.semaphore_signal(more_relayed, inc=1, device_id={"shard": mirror(asked, n_devs)}, device_id_type=pl.DeviceIdType.MESH)
+
+                @pl.when(jnp.logical_not(is_low(asked, n_devs)))
+                def _():
+                    pl.semaphore_signal(more_own, inc=1, device_id={"shard": asked}, device_id_type=pl.DeviceIdType.MESH)
+
+        def stratum_body(stratum, begins=False, moving=False, ends=False):
+            if not begins:
                 slot_in = stratum % n_devs
                 arrival(leaving.at[0], arriving.at[slot_in], hop_recv.at[slot_in]).wait()
-
-            @pl.when(jnp.logical_and(stratum > 0, stratum <= n_devs - k))
-            def _():
+            if moving:
                 wait_block((first - stratum + n_devs) % n_devs)
-
-            if not ends:
-                asked = (first - stratum - AHEAD + 2 * n_devs) % n_devs
-
-                @pl.when(jnp.logical_and(stratum > 0, jnp.logical_and(stratum + AHEAD <= n_devs - k, asked != me)))
-                def _():
-                    @pl.when(is_low(asked, n_devs))
-                    def _():
-                        pl.semaphore_signal(more_relayed, inc=1, device_id={"shard": mirror(asked, n_devs)}, device_id_type=pl.DeviceIdType.MESH)
-
-                    @pl.when(jnp.logical_not(is_low(asked, n_devs)))
-                    def _():
-                        pl.semaphore_signal(more_own, inc=1, device_id={"shard": asked}, device_id_type=pl.DeviceIdType.MESH)
+                ask(stratum + AHEAD)
 
             for s in range(SLOTS):
-                slot(work_of(s, stratum, ends), None if ends else send_user)
-
-        def send_user(stratum):
+                slot(work_of(s, stratum, ends), None if ends else functools.partial(send_user, begins))
+
+        def send_user(begins, stratum):
             hop(stratum).start()
-
-            @pl.when(stratum > 0)
-            def _():
+            if not begins:
                 hop(stratum - 1).wait_send()
 
         for s in range(-LEAD * last, 0):
@@ -352,12 +355,18 @@
             some = rated.at[first + c, :, pl.ds(0, last * items)]
             arrival(some, some, block_recv.at[first + c]).wait()
 
-        @pl.loop(0, strata - 1)
+        stratum_body(0, begins=True)
+
+        @pl.loop(1, n_devs - k + 1)
         def _(stratum):
-            stratum_body(stratum, False)
+            stratum_body(stratum, moving=True)
+
+        @pl.loop(n_devs - k + 1, strata - 1)
+        def _(stratum):
+            stratum_body(stratum)
 
         hop(strata - 2).wait_send()
-        stratum_body(strata - 1, True)
+        stratum_body(strata - 1, ends=True)
 
         def end_copies(c):
             done = handed.at[c] if c < last else leaving.at[(strata - 1) % 2]
@@ -376,10 +385,6 @@
             for copy in end_copies(c):
                 wait_sent(*copy)
 
-    wait_sent(*user_copy)
-    wait_sent(*item_copy)
-
-    wait_sent(*part_copy(0))
 
     @pl.when(home != me)
     def _():

time: 753 us -> 755 us (level)
  no operation moved by 1% of the time
where the time goes in v10:
time: 755 us
  Pallas kernels  751 us (99%)
    pallas_call x1, Pallas kernels, local(): pl.pallas_call(functools.partial(kernel, n_devs, EPOCHS * n_devs, step_si...  751 us

profile of v10, /device:TPU:39, one launch (start us, length us, event | category | flops | bytes accessed | tf_op | source)
XLA Modules:
  0.0 754.6 jit_solution(7435986495840559606)
XLA Ops:
  0.6 750.9 %strata.1 = (f32[64,192]{1,0:T(8,128)}, f32[192,128]{1,0:T(8,128)}) custom-call(f32[64,16384]{1,0:T(8,128)} %ratings.1, s32[64,16384]{1,0:T(8,128)} %observed.1, f32[64,192]{1,0:T(8,128)} %user_init.1, f32[192,128]{1,0:T(8,128)} %bitcast.2), custom_call_target="tpu_custom_call" | custom-call | tf_op jit(solution)/shard_map/strata/pallas_call | solution.py:437
  751.6 1.5 copy.8
  753.1 1.5 copy.9

commit v11 on v10

--- a/solution.py
+++ b/solution.py
@@ -19,6 +19,19 @@
 
 ROW_BY_ROW = (((1,), (1,)), ((), ()))
 PLAIN = (((1,), (0,)), ((), ()))
+
+
+LANES = 128
+
+
+def rounded(first, second, pair):
+    return jnp.concatenate([first[pair], second[pair]], axis=1)
+
+
+def keep_rounded(first, second, pair, values):
+    values = values.astype(jnp.bfloat16)
+    first[pair] = values[:, :LANES]
+    second[pair] = values[:, LANES:]
 
 
 def dot(lhs, rhs, dims):
@@ -65,7 +78,7 @@
 
 def kernel(n_devs, strata, step_size, weight_decay, ratings, observed, user_init, item_init, user_out, item_out,
            masked, seen, rated, turned,
-           arriving, handed, handed_bf, leaving, user, user_bf, item, item_bf, user_start, item_start,
+           arriving, handed, handed_bf, handed_bf_2, leaving, user, user_bf, user_bf_2, item, item_bf, item_bf_2, user_start, item_start,
            ratings_here, seen_here, go, more_own, more_relayed, relay_send, first_send, first_recv, block_send, block_recv,
            start_send, user_recv, item_recv, hop_send, hop_recv, end_send, end_recv):
     k = ITEM_BLOCKS
@@ -160,13 +173,6 @@
     @pl.loop(1, SOON)
     def _(turn):
         mask(turn)
-
-    wait_sent(*user_copy)
-    wait_sent(*item_copy)
-    wait_sent(*part_copy(0))
-
-    @pl.loop(1, SOON)
-    def _(turn):
         send(*block_copy(turn))
 
     def send_up():
@@ -246,22 +252,22 @@
                 arriving[0] = user_start[0]
             else:
                 handed[c - 1] = user_start[c]
-                handed_bf[c - 1] = user_start[c].astype(jnp.bfloat16)
+                keep_rounded(handed_bf, handed_bf_2, c - 1, user_start[c])
             item[c] = item_start[c].T
-            item_bf[c] = item[c].astype(jnp.bfloat16)
+            keep_rounded(item_bf, item_bf_2, c, item_start[c].T)
 
         def steps_of(c, half, stratum, send_user):
             kept = {}
 
             def predict():
                 if half == 0:
-                    lhs = arriving[stratum % n_devs].astype(jnp.bfloat16) if c == 0 else handed_bf[c - 1]
+                    lhs = arriving[stratum % n_devs].astype(jnp.bfloat16) if c == 0 else rounded(handed_bf, handed_bf_2, c - 1)
                 else:
-                    lhs = user_bf[c]
+                    lhs = rounded(user_bf, user_bf_2, c)
                 if half % 2 == 0:
-                    kept["predicted"] = dot(lhs, item_bf[c], ROW_BY_ROW)
+                    kept["predicted"] = dot(lhs, rounded(item_bf, item_bf_2, c), ROW_BY_ROW)
                 else:
-                    kept["predicted"] = dot(item_bf[c], lhs, ROW_BY_ROW)
+                    kept["predicted"] = dot(rounded(item_bf, item_bf_2, c), lhs, ROW_BY_ROW)
 
             def descend():
                 if half % 2 == 0:
@@ -272,7 +278,11 @@
                 else:
                     known = turned[c]
                 residual = jnp.where(known != known, 0.0, kept["predicted"] - known).astype(jnp.bfloat16)
-                kept["grad"] = dot(residual, item_bf[c] if half % 2 == 0 else user_bf[c], PLAIN)
+                kept["grad"] = dot(
+                    residual,
+                    rounded(item_bf, item_bf_2, c) if half % 2 == 0 else rounded(user_bf, user_bf_2, c),
+                    PLAIN,
+                )
 
             def update():
                 if half % 2 == 0:
@@ -285,17 +295,16 @@
                 else:
                     old = item[c]
                 new = old * (1 - step_size * weight_decay) - step_size * kept["grad"]
-                new_bf = new.astype(jnp.bfloat16)
                 if half % 2 == 1:
                     item[c] = new
-                    item_bf[c] = new_bf
+                    keep_rounded(item_bf, item_bf_2, c, new)
                     return
-                user_bf[c] = new_bf
+                keep_rounded(user_bf, user_bf_2, c, new)
                 if half < HALF_STEPS - 2:
                     user[c] = new
                 elif c < last:
                     handed[c] = new
-                    handed_bf[c] = new_bf
+                    keep_rounded(handed_bf, handed_bf_2, c, new)
                 else:
                     leaving[stratum % 2] = new
                     if send_user is not None:
@@ -385,6 +394,10 @@
             for copy in end_copies(c):
                 wait_sent(*copy)
 
+
+    wait_sent(*user_copy)
+    wait_sent(*item_copy)
+    wait_sent(*part_copy(0))
 
     @pl.when(home != me)
     def _():
@@ -446,12 +459,15 @@
                 pltpu.VMEM((k, items, users), jnp.float32),
                 pltpu.VMEM((n_devs, users, rank), jnp.float32),
                 pltpu.VMEM((k - 1, users, rank), jnp.float32),
-                pltpu.VMEM((k - 1, users, rank), jnp.bfloat16),
+                pltpu.VMEM((k - 1, users, LANES), jnp.bfloat16),
+                pltpu.VMEM((k - 1, users, rank - LANES), jnp.bfloat16),
                 pltpu.VMEM((2, users, rank), jnp.float32),
                 pltpu.VMEM((k, users, rank), jnp.float32),
-                pltpu.VMEM((k, users, rank), jnp.bfloat16),
+                pltpu.VMEM((k, users, LANES), jnp.bfloat16),
+                pltpu.VMEM((k, users, rank - LANES), jnp.bfloat16),
                 pltpu.VMEM((k, items, rank), jnp.float32),
-                pltpu.VMEM((k, items, rank), jnp.bfloat16),
+                pltpu.VMEM((k, items, LANES), jnp.bfloat16),
+                pltpu.VMEM((k, items, rank - LANES), jnp.bfloat16),
                 pltpu.VMEM((k, users, rank), jnp.float32),
                 pltpu.VMEM((k, rank, items), jnp.float32),
                 dma((workers,)),

time: 755 us -> 760 us (level)
  no operation moved by 1% of the time
where the time goes in v11:
time: 760 us
  Pallas kernels  756 us (99%)
    pallas_call x1, Pallas kernels, local(): pl.pallas_call(functools.partial(kernel, n_devs, EPOCHS * n_devs, step_si...  756 us

profile of v11, /device:TPU:39, one launch (start us, length us, event | category | flops | bytes accessed | tf_op | source)
XLA Modules:
  0.0 759.8 jit_solution(8862959043151464671)
XLA Ops:
  0.6 756.2 %strata.1 = (f32[64,192]{1,0:T(8,128)}, f32[192,128]{1,0:T(8,128)}) custom-call(f32[64,16384]{1,0:T(8,128)} %ratings.1, s32[64,16384]{1,0:T(8,128)} %observed.1, f32[64,192]{1,0:T(8,128)} %user_init.1, f32[192,128]{1,0:T(8,128)} %bitcast.2), custom_call_target="tpu_custom_call" | custom-call | tf_op jit(solution)/shard_map/strata/pallas_call | solution.py:450
  756.8 1.5 copy.8
  758.3 1.5 copy.9

commit v12 on v10

--- a/solution.py
+++ b/solution.py
@@ -12,6 +12,7 @@
 EPOCHS = 2
 ITEM_BLOCKS = 4
 SLOTS = 9
+UNASKED = 8
 AHEAD = 12
 SOON = 2
 HALF_STEPS = 2 * STRATUM_STEPS
@@ -66,7 +67,7 @@
 def kernel(n_devs, strata, step_size, weight_decay, ratings, observed, user_init, item_init, user_out, item_out,
            masked, seen, rated, turned,
            arriving, handed, handed_bf, leaving, user, user_bf, item, item_bf, user_start, item_start,
-           ratings_here, seen_here, go, more_own, more_relayed, relay_send, first_send, first_recv, block_send, block_recv,
+           ratings_here, seen_here, more_own, more_relayed, relay_send, first_send, first_recv, block_send, block_recv,
            start_send, user_recv, item_recv, hop_send, hop_recv, end_send, end_recv):
     k = ITEM_BLOCKS
     workers = n_devs // k
@@ -196,14 +197,16 @@
         def _(turn):
             mask(turn)
 
-        pl.semaphore_wait(go, 1)
+        @pl.loop(1, SOON)
+        def _(turn):
+            wait_sent(*block_copy(turn))
 
         @pl.loop(SOON, workers)
         def _(turn):
             to, _ = columns_of(across, turn)
             relays = to != across
 
-            @pl.when(turn * k - me % k > AHEAD)
+            @pl.when(turn * k - me % k > UNASKED)
             def _():
                 pl.semaphore_wait(more_own, 1)
 
@@ -236,11 +239,21 @@
             arrival(item_init, item_start.at[c], item_recv.at[c]).wait()
             part = rated.at[first + c, :, c * items : (c + 1) * items]
             arrival(part, part, first_recv.at[c]).wait()
-        for c in range(k):
-            @pl.when(jnp.logical_not(is_low(first + c, n_devs)))
-            def _():
-                pl.semaphore_signal(go, inc=1, device_id={"shard": first + c}, device_id_type=pl.DeviceIdType.MESH)
-
+        def ask(stratum):
+            asked = (first - stratum + 2 * n_devs) % n_devs
+
+            @pl.when(jnp.logical_and(stratum <= n_devs - k, asked != me))
+            def _():
+                @pl.when(is_low(asked, n_devs))
+                def _():
+                    pl.semaphore_signal(more_relayed, inc=1, device_id={"shard": mirror(asked, n_devs)}, device_id_type=pl.DeviceIdType.MESH)
+
+                @pl.when(jnp.logical_not(is_low(asked, n_devs)))
+                def _():
+                    pl.semaphore_signal(more_own, inc=1, device_id={"shard": asked}, device_id_type=pl.DeviceIdType.MESH)
+
+        for stratum in range(UNASKED + 1, AHEAD + 1):
+            ask(stratum)
         for c in range(k):
             if c == 0:
                 arriving[0] = user_start[0]
@@ -319,19 +332,6 @@
                     work.append((c, place % SLOTS, stratum + place // SLOTS))
             return work
 
-        def ask(stratum):
-            asked = (first - stratum + 2 * n_devs) % n_devs
-
-            @pl.when(jnp.logical_and(stratum <= n_devs - k, asked != me))
-            def _():
-                @pl.when(is_low(asked, n_devs))
-                def _():
-                    pl.semaphore_signal(more_relayed, inc=1, device_id={"shard": mirror(asked, n_devs)}, device_id_type=pl.DeviceIdType.MESH)
-
-                @pl.when(jnp.logical_not(is_low(asked, n_devs)))
-                def _():
-                    pl.semaphore_signal(more_own, inc=1, device_id={"shard": asked}, device_id_type=pl.DeviceIdType.MESH)
-
         def stratum_body(stratum, begins=False, moving=False, ends=False):
             if not begins:
                 slot_in = stratum % n_devs
@@ -391,12 +391,12 @@
         some = rated.at[me, :, pl.ds(0, last * items)]
         arrival(some, some, block_send.at[0]).wait()
 
-    @pl.loop(1, SOON)
-    def _(turn):
-        wait_sent(*block_copy(turn))
-
     @pl.when(low)
     def _():
+        @pl.loop(1, SOON)
+        def _(turn):
+            wait_sent(*block_copy(turn))
+
         @pl.loop(SOON, workers)
         def _(turn):
             to, _ = columns_of(me, turn)
@@ -458,7 +458,6 @@
                 dma((workers,)),
                 pltpu.SemaphoreType.REGULAR,
                 pltpu.SemaphoreType.REGULAR,
-                pltpu.SemaphoreType.REGULAR,
                 dma((workers,)),
                 dma,
                 dma((k,)),

time: 755 us -> 752 us (level)
  no operation moved by 1% of the time
where the time goes in v12:
time: 752 us
  Pallas kernels  748 us (99%)
    pallas_call x1, Pallas kernels, local(): pl.pallas_call(functools.partial(kernel, n_devs, EPOCHS * n_devs, step_si...  748 us

profile of v12, /device:TPU:39, one launch (start us, length us, event | category | flops | bytes accessed | tf_op | source)
XLA Modules:
  0.0 751.6 jit_solution(6351303419934664168)
XLA Ops:
  0.6 748.0 %strata.1 = (f32[64,192]{1,0:T(8,128)}, f32[192,128]{1,0:T(8,128)}) custom-call(f32[64,16384]{1,0:T(8,128)} %ratings.1, s32[64,16384]{1,0:T(8,128)} %observed.1, f32[64,192]{1,0:T(8,128)} %user_init.1, f32[192,128]{1,0:T(8,128)} %bitcast.2), custom_call_target="tpu_custom_call" | custom-call | tf_op jit(solution)/shard_map/strata/pallas_call | solution.py:437
  748.6 1.5 copy.8
  750.1 1.5 copy.9

commit v13 on v12

--- a/solution.py
+++ b/solution.py
@@ -336,17 +336,16 @@
             if not begins:
                 slot_in = stratum % n_devs
                 arrival(leaving.at[0], arriving.at[slot_in], hop_recv.at[slot_in]).wait()
+                hop(stratum - 1).wait_send()
             if moving:
                 wait_block((first - stratum + n_devs) % n_devs)
                 ask(stratum + AHEAD)
 
             for s in range(SLOTS):
-                slot(work_of(s, stratum, ends), None if ends else functools.partial(send_user, begins))
-
-        def send_user(begins, stratum):
+                slot(work_of(s, stratum, ends), None if ends else send_user)
+
+        def send_user(stratum):
             hop(stratum).start()
-            if not begins:
-                hop(stratum - 1).wait_send()
 
         for s in range(-LEAD * last, 0):
             slot(work_of(s, 0))
@@ -365,7 +364,6 @@
         def _(stratum):
             stratum_body(stratum)
 
-        hop(strata - 2).wait_send()
         stratum_body(strata - 1, ends=True)
 
         def end_copies(c):

time: 752 us -> 752 us (level)
  no operation moved by 1% of the time
where the time goes in v13:
time: 752 us
  Pallas kernels  748 us (99%)
    pallas_call x1, Pallas kernels, local(): pl.pallas_call(functools.partial(kernel, n_devs, EPOCHS * n_devs, step_si...  748 us

profile of v13, /device:TPU:39, one launch (start us, length us, event | category | flops | bytes accessed | tf_op | source)
XLA Modules:
  0.0 752.1 jit_solution(16109637323981107621)
XLA Ops:
  0.6 748.4 %strata.1 = (f32[64,192]{1,0:T(8,128)}, f32[192,128]{1,0:T(8,128)}) custom-call(f32[64,16384]{1,0:T(8,128)} %ratings.1, s32[64,16384]{1,0:T(8,128)} %observed.1, f32[64,192]{1,0:T(8,128)} %user_init.1, f32[192,128]{1,0:T(8,128)} %bitcast.2), custom_call_target="tpu_custom_call" | custom-call | tf_op jit(solution)/shard_map/strata/pallas_call | solution.py:435
  749.1 1.5 copy.8
  750.6 1.5 copy.9

commit v14 on v13

--- a/solution.py
+++ b/solution.py
@@ -267,14 +267,17 @@
             kept = {}
 
             def predict():
-                if half == 0:
-                    lhs = arriving[stratum % n_devs].astype(jnp.bfloat16) if c == 0 else handed_bf[c - 1]
+                items_now = fresh.pop(("item", c)) if ("item", c) in fresh else item_bf[c]
+                if half == 0 and c == 0:
+                    users_now = arriving[stratum % n_devs].astype(jnp.bfloat16)
+                elif half == 0:
+                    users_now = fresh.pop(("handed", c)) if ("handed", c) in fresh else handed_bf[c - 1]
                 else:
-                    lhs = user_bf[c]
+                    users_now = fresh.pop(("user", c)) if ("user", c) in fresh else user_bf[c]
                 if half % 2 == 0:
-                    kept["predicted"] = dot(lhs, item_bf[c], ROW_BY_ROW)
+                    kept["predicted"] = dot(users_now, items_now, ROW_BY_ROW)
                 else:
-                    kept["predicted"] = dot(item_bf[c], lhs, ROW_BY_ROW)
+                    kept["predicted"] = dot(items_now, users_now, ROW_BY_ROW)
 
             def descend():
                 if half % 2 == 0:
@@ -302,19 +305,24 @@
                 if half % 2 == 1:
                     item[c] = new
                     item_bf[c] = new_bf
+                    fresh["item", c] = new_bf
                     return
                 user_bf[c] = new_bf
+                fresh["user", c] = new_bf
                 if half < HALF_STEPS - 2:
                     user[c] = new
                 elif c < last:
                     handed[c] = new
                     handed_bf[c] = new_bf
+                    fresh["handed", c + 1] = new_bf
                 else:
                     leaving[stratum % 2] = new
                     if send_user is not None:
                         send_user(stratum)
 
             return predict, descend, update
+
+        fresh = {}
 
         def slot(work, send_user=None):
             steps = [steps_of(c, half, stratum, send_user) for c, half, stratum in reversed(work)]
@@ -341,8 +349,10 @@
                 wait_block((first - stratum + n_devs) % n_devs)
                 ask(stratum + AHEAD)
 
+            fresh.clear()
             for s in range(SLOTS):
                 slot(work_of(s, stratum, ends), None if ends else send_user)
+            fresh.clear()
 
         def send_user(stratum):
             hop(stratum).start()

time: 752 us -> 751 us (level)
  no operation moved by 1% of the time
where the time goes in v14:
time: 751 us; the launch traced here: 749 us
  Pallas kernels  746 us (99%)
    pallas_call x1, Pallas kernels, local(): pl.pallas_call(functools.partial(kernel, n_devs, EPOCHS * n_devs, step_si...  746 us

profile of v14, /device:TPU:39, one launch (start us, length us, event | category | flops | bytes accessed | tf_op | source)
XLA Modules:
  0.0 749.5 jit_solution(1862113099206054928)
XLA Ops:
  0.6 745.8 %strata.1 = (f32[64,192]{1,0:T(8,128)}, f32[192,128]{1,0:T(8,128)}) custom-call(f32[64,16384]{1,0:T(8,128)} %ratings.1, s32[64,16384]{1,0:T(8,128)} %observed.1, f32[64,192]{1,0:T(8,128)} %user_init.1, f32[192,128]{1,0:T(8,128)} %bitcast.2), custom_call_target="tpu_custom_call" | custom-call | tf_op jit(solution)/shard_map/strata/pallas_call | solution.py:445
  746.4 1.5 copy.8
  747.9 1.5 copy.9

commit v15 on v14

--- a/solution.py
+++ b/solution.py
@@ -29,12 +29,13 @@
 def worker_device(worker, n_devs):
     if n_devs != 128:
         return worker
-    plane = worker // 16
-    place = worker + plane * (31 - 2 * worker)
-    y = place // 4
-    odd = y % 2
-    x = place % 4
-    x = x + odd * (3 - 2 * x)
+    quarter = worker // 8
+    row = worker % 8 // 2
+    y = row + quarter % 2 * (3 - 2 * row)
+    far = (row + worker) % 2
+    half = quarter // 2
+    x = 1 - far + half * (1 + 2 * far)
+    plane = (quarter + half) % 2
     return ((plane * 4 + y) * 4 + x) * 2 + 1
 
 
@@ -45,8 +46,11 @@
     plane = (chip // 16) % 2
     y = (chip // 4) % 4
     x = chip % 4
-    place = y * 4 + x + (y % 2) * (3 - 2 * x)
-    return place + plane * (31 - 2 * place)
+    half = x // 2
+    quarter = 2 * half + (plane + half) % 2
+    row = y + quarter % 2 * (3 - 2 * y)
+    far = 1 - x + half * (2 * x - 3)
+    return 8 * quarter + 2 * row + (far + row) % 2
 
 
 def is_worker(dev, n_devs):

time: 751 us -> 753 us (level)
  no operation moved by 1% of the time
where the time goes in v15:
time: 753 us; the launch traced here: 749 us
  Pallas kernels  746 us (99%)
    pallas_call x1, Pallas kernels, local(): pl.pallas_call(functools.partial(kernel, n_devs, EPOCHS * n_devs, step_si...  746 us

profile of v15, /device:TPU:39, one launch (start us, length us, event | category | flops | bytes accessed | tf_op | source)
XLA Modules:
  0.0 749.3 jit_solution(2632244183270760247)
XLA Ops:
  0.6 745.7 %strata.1 = (f32[64,192]{1,0:T(8,128)}, f32[192,128]{1,0:T(8,128)}) custom-call(f32[64,16384]{1,0:T(8,128)} %ratings.1, s32[64,16384]{1,0:T(8,128)} %observed.1, f32[64,192]{1,0:T(8,128)} %user_init.1, f32[192,128]{1,0:T(8,128)} %bitcast.2), custom_call_target="tpu_custom_call" | custom-call | tf_op jit(solution)/shard_map/strata/pallas_call | solution.py:449
  746.3 1.5 copy.8
  747.8 1.5 copy.9

commit v16 on v14

--- a/solution.py
+++ b/solution.py
@@ -277,7 +277,9 @@
                 if half % 2 == 0:
                     kept["predicted"] = dot(users_now, items_now, ROW_BY_ROW)
                 else:
-                    kept["predicted"] = dot(items_now, users_now, ROW_BY_ROW)
+                    kept["predicted"] = jnp.concatenate(
+                        [dot(items_now[r : r + items // 2], users_now, ROW_BY_ROW) for r in (0, items // 2)], axis=0
+                    )
 
             def descend():
                 if half % 2 == 0:
@@ -288,7 +290,11 @@
                 else:
                     known = turned[c]
                 residual = jnp.where(known != known, 0.0, kept["predicted"] - known).astype(jnp.bfloat16)
-                kept["grad"] = dot(residual, item_bf[c] if half % 2 == 0 else user_bf[c], PLAIN)
+                if half % 2 == 0:
+                    kept["grad"] = dot(residual, item_bf[c], PLAIN)
+                else:
+                    rows = items // 2
+                    kept["grad"] = jnp.concatenate([dot(residual[r : r + rows], user_bf[c], PLAIN) for r in (0, rows)], axis=0)
 
             def update():
                 if half % 2 == 0:
@@ -318,16 +324,18 @@
                 else:
                     leaving[stratum % 2] = new
                     if send_user is not None:
-                        send_user(stratum)
+                        send_user()
 
             return predict, descend, update
 
         fresh = {}
 
-        def slot(work, send_user=None):
+        def slot(work, send_user=None, await_user=None):
             steps = [steps_of(c, half, stratum, send_user) for c, half, stratum in reversed(work)]
-            for step in zip(*steps):
-                for of_pair in step:
+            for number, step in enumerate(zip(*steps)):
+                for place, of_pair in enumerate(step):
+                    if number == 0 and place == len(step) - 1 and await_user is not None:
+                        await_user()
                     of_pair()
 
         def work_of(s, stratum, first_only=False):
@@ -341,21 +349,24 @@
             return work
 
         def stratum_body(stratum, begins=False, moving=False, ends=False):
-            if not begins:
+            def await_user():
                 slot_in = stratum % n_devs
                 arrival(leaving.at[0], arriving.at[slot_in], hop_recv.at[slot_in]).wait()
+
+            if not begins:
                 hop(stratum - 1).wait_send()
             if moving:
                 wait_block((first - stratum + n_devs) % n_devs)
-                ask(stratum + AHEAD)
+
+            def send_on():
+                hop(stratum).start()
+                if moving:
+                    ask(stratum + AHEAD)
 
             fresh.clear()
             for s in range(SLOTS):
-                slot(work_of(s, stratum, ends), None if ends else send_user)
+                slot(work_of(s, stratum, ends), None if ends else send_on, await_user if s == 0 and not begins else None)
             fresh.clear()
-
-        def send_user(stratum):
-            hop(stratum).start()
 
         for s in range(-LEAD * last, 0):
             slot(work_of(s, 0))

time: 751 us -> 755 us (level)
  no operation moved by 1% of the time
where the time goes in v16:
time: 755 us
  Pallas kernels  751 us (99%)
    pallas_call x1, Pallas kernels, local(): pl.pallas_call(functools.partial(kernel, n_devs, EPOCHS * n_devs, step_si...  751 us

profile of v16, /device:TPU:39, one launch (start us, length us, event | category | flops | bytes accessed | tf_op | source)
XLA Modules:
  0.0 754.6 jit_solution(15666398202502887205)
XLA Ops:
  0.6 750.9 %strata.1 = (f32[64,192]{1,0:T(8,128)}, f32[192,128]{1,0:T(8,128)}) custom-call(f32[64,16384]{1,0:T(8,128)} %ratings.1, s32[64,16384]{1,0:T(8,128)} %observed.1, f32[64,192]{1,0:T(8,128)} %user_init.1, f32[192,128]{1,0:T(8,128)} %bitcast.2), custom_call_target="tpu_custom_call" | custom-call | tf_op jit(solution)/shard_map/strata/pallas_call | solution.py:456
  751.6 1.5 copy.8
  753.1 1.5 copy.9

commit v17 on v14

--- a/solution.py
+++ b/solution.py
@@ -318,7 +318,7 @@
                 else:
                     leaving[stratum % 2] = new
                     if send_user is not None:
-                        send_user(stratum)
+                        send_user()
 
             return predict, descend, update
 
@@ -341,21 +341,25 @@
             return work
 
         def stratum_body(stratum, begins=False, moving=False, ends=False):
+            def send_user():
+                hop(stratum).start()
+                if not begins:
+                    hop(stratum - 1).wait_send()
+                if moving:
+                    ask(stratum + AHEAD)
+
             if not begins:
                 slot_in = stratum % n_devs
                 arrival(leaving.at[0], arriving.at[slot_in], hop_recv.at[slot_in]).wait()
+            if ends:
                 hop(stratum - 1).wait_send()
             if moving:
                 wait_block((first - stratum + n_devs) % n_devs)
-                ask(stratum + AHEAD)
 
             fresh.clear()
             for s in range(SLOTS):
                 slot(work_of(s, stratum, ends), None if ends else send_user)
             fresh.clear()
-
-        def send_user(stratum):
-            hop(stratum).start()
 
         for s in range(-LEAD * last, 0):
             slot(work_of(s, 0))

time: 751 us -> 749 us (level)
  no operation moved by 1% of the time
where the time goes in v17:
time: 749 us; the launch traced here: 748 us
  Pallas kernels  745 us (99%)
    pallas_call x1, Pallas kernels, local(): pl.pallas_call(functools.partial(kernel, n_devs, EPOCHS * n_devs, step_si...  745 us

profile of v17, /device:TPU:39, one launch (start us, length us, event | category | flops | bytes accessed | tf_op | source)
XLA Modules:
  0.0 748.2 jit_solution(16905224373723374012)
XLA Ops:
  0.6 744.6 %strata.1 = (f32[64,192]{1,0:T(8,128)}, f32[192,128]{1,0:T(8,128)}) custom-call(f32[64,16384]{1,0:T(8,128)} %ratings.1, s32[64,16384]{1,0:T(8,128)} %observed.1, f32[64,192]{1,0:T(8,128)} %user_init.1, f32[192,128]{1,0:T(8,128)} %bitcast.2), custom_call_target="tpu_custom_call" | custom-call | tf_op jit(solution)/shard_map/strata/pallas_call | solution.py:449
  745.2 1.5 copy.8
  746.7 1.5 copy.9

commit v18 on v17

--- a/solution.py
+++ b/solution.py
@@ -20,6 +20,18 @@
 
 ROW_BY_ROW = (((1,), (1,)), ((), ()))
 PLAIN = (((1,), (0,)), ((), ()))
+
+
+LANES = 128
+
+
+def joined(first, second, place):
+    return jnp.concatenate([first[place], second[place]], axis=1)
+
+
+def put(first, second, place, values):
+    first[place] = values[:, :LANES]
+    second[place] = values[:, LANES:]
 
 
 def dot(lhs, rhs, dims):
@@ -66,9 +78,9 @@
 
 def kernel(n_devs, strata, step_size, weight_decay, ratings, observed, user_init, item_init, user_out, item_out,
            masked, seen, rated, turned,
-           arriving, handed, handed_bf, leaving, user, user_bf, item, item_bf, user_start, item_start,
+           arriving, arriving_2, handed, handed_bf, leaving, leaving_2, user, user_bf, item, item_bf, user_start, item_start,
            ratings_here, seen_here, more_own, more_relayed, relay_send, first_send, first_recv, block_send, block_recv,
-           start_send, user_recv, item_recv, hop_send, hop_recv, end_send, end_recv):
+           start_send, user_recv, item_recv, hop_send, hop_recv, hop_send_2, hop_recv_2, end_send, end_recv):
     k = ITEM_BLOCKS
     workers = n_devs // k
     items = item_init.shape[1]
@@ -231,8 +243,11 @@
             arrival(rated.at[block], rated.at[block], block_recv.at[block]).wait()
 
         def hop(stratum):
-            slot = (stratum + 1) % n_devs
-            return remote(leaving.at[stratum % 2], arriving.at[slot], hop_send.at[stratum % 2], hop_recv.at[slot], after)
+            here, there = stratum % 2, (stratum + 1) % n_devs
+            return (
+                remote(leaving.at[here], arriving.at[there], hop_send.at[here], hop_recv.at[there], after),
+                remote(leaving_2.at[here], arriving_2.at[there], hop_send_2.at[here], hop_recv_2.at[there], after),
+            )
 
         for c in range(k):
             arrival(user_init, user_start.at[c], user_recv.at[c]).wait()
@@ -256,7 +271,7 @@
             ask(stratum)
         for c in range(k):
             if c == 0:
-                arriving[0] = user_start[0]
+                put(arriving, arriving_2, 0, user_start[0])
             else:
                 handed[c - 1] = user_start[c]
                 handed_bf[c - 1] = user_start[c].astype(jnp.bfloat16)
@@ -269,7 +284,8 @@
             def predict():
                 items_now = fresh.pop(("item", c)) if ("item", c) in fresh else item_bf[c]
                 if half == 0 and c == 0:
-                    users_now = arriving[stratum % n_devs].astype(jnp.bfloat16)
+                    kept["arrived"] = joined(arriving, arriving_2, stratum % n_devs)
+                    users_now = kept["arrived"].astype(jnp.bfloat16)
                 elif half == 0:
                     users_now = fresh.pop(("handed", c)) if ("handed", c) in fresh else handed_bf[c - 1]
                 else:
@@ -295,7 +311,7 @@
                     if half > 0:
                         old = user[c]
                     elif c == 0:
-                        old = arriving[stratum % n_devs]
+                        old = kept["arrived"]
                     else:
                         old = handed[c - 1]
                 else:
@@ -316,7 +332,7 @@
                     handed_bf[c] = new_bf
                     fresh["handed", c + 1] = new_bf
                 else:
-                    leaving[stratum % 2] = new
+                    put(leaving, leaving_2, stratum % 2, new)
                     if send_user is not None:
                         send_user()
 
@@ -342,17 +358,21 @@
 
         def stratum_body(stratum, begins=False, moving=False, ends=False):
             def send_user():
-                hop(stratum).start()
+                for copy in hop(stratum):
+                    copy.start()
                 if not begins:
-                    hop(stratum - 1).wait_send()
+                    for copy in hop(stratum - 1):
+                        copy.wait_send()
                 if moving:
                     ask(stratum + AHEAD)
 
             if not begins:
                 slot_in = stratum % n_devs
                 arrival(leaving.at[0], arriving.at[slot_in], hop_recv.at[slot_in]).wait()
+                arrival(leaving_2.at[0], arriving_2.at[slot_in], hop_recv_2.at[slot_in]).wait()
             if ends:
-                hop(stratum - 1).wait_send()
+                for copy in hop(stratum - 1):
+                    copy.wait_send()
             if moving:
                 wait_block((first - stratum + n_devs) % n_devs)
 
@@ -381,13 +401,14 @@
         stratum_body(strata - 1, ends=True)
 
         def end_copies(c):
-            done = handed.at[c] if c < last else leaving.at[(strata - 1) % 2]
+            done = handed.at[c] if c < last else user_start.at[last]
             block = first + c
             return (
                 (done, user_out, end_send.at[2 * c], end_recv.at[0], (block + 1) % n_devs),
                 (item_start.at[c], item_out, end_send.at[2 * c + 1], end_recv.at[1], block),
             )
 
+        user_start[last] = joined(leaving, leaving_2, (strata - 1) % 2)
         for c in range(k):
             item_start[c] = item[c].T
         for c in range(k):
@@ -456,10 +477,12 @@
                 pltpu.VMEM((users, n_devs * items), jnp.int32),
                 pltpu.VMEM((n_devs, users, wide), jnp.float32),
                 pltpu.VMEM((k, items, users), jnp.float32),
-                pltpu.VMEM((n_devs, users, rank), jnp.float32),
+                pltpu.VMEM((n_devs, users, LANES), jnp.float32),
+                pltpu.VMEM((n_devs, users, rank - LANES), jnp.float32),
                 pltpu.VMEM((k - 1, users, rank), jnp.float32),
                 pltpu.VMEM((k - 1, users, rank), jnp.bfloat16),
-                pltpu.VMEM((2, users, rank), jnp.float32),
+                pltpu.VMEM((2, users, LANES), jnp.float32),
+                pltpu.VMEM((2, users, rank - LANES), jnp.float32),
                 pltpu.VMEM((k, users, rank), jnp.float32),
                 pltpu.VMEM((k, users, rank), jnp.bfloat16),
                 pltpu.VMEM((k, items, rank), jnp.float32),
@@ -480,6 +503,8 @@
                 dma((k,)),
                 dma((2,)),
                 dma((n_devs,)),
+                dma((2,)),
+                dma((n_devs,)),
                 dma((2 * k,)),
                 dma((2,)),
             ],

time: 749 us -> 750 us (level)
  no operation moved by 1% of the time
where the time goes in v18:
time: 750 us
  Pallas kernels  746 us (99%)
    pallas_call x1, Pallas kernels, local(): pl.pallas_call(functools.partial(kernel, n_devs, EPOCHS * n_devs, step_si...  746 us

profile of v18, /device:TPU:39, one launch (start us, length us, event | category | flops | bytes accessed | tf_op | source)
XLA Modules:
  0.0 749.5 jit_solution(2372186880190955297)
XLA Ops:
  0.6 745.9 %strata.1 = (f32[64,192]{1,0:T(8,128)}, f32[192,128]{1,0:T(8,128)}) custom-call(f32[64,16384]{1,0:T(8,128)} %ratings.1, s32[64,16384]{1,0:T(8,128)} %observed.1, f32[64,192]{1,0:T(8,128)} %user_init.1, f32[192,128]{1,0:T(8,128)} %bitcast.2), custom_call_target="tpu_custom_call" | custom-call | tf_op jit(solution)/shard_map/strata/pallas_call | solution.py:470
  746.5 1.5 copy.8
  748.0 1.5 copy.9
